TPU v7x, 8 devices: a whole 2x2x1 slice. The times are simulated.
8 devices in a mesh: dp: 1 (over z), tp: 2 (over y), ep: 4 (over x, core).
Axes of the slice: x: 2, y: 2, z: 1, core: 2. Of those that a mesh axis runs over, the one named last changes fastest.
Arguments:
- tokens: bfloat16 [1024, 1024], P(('dp', 'ep'))
- grad_out: bfloat16 [1024, 1024], P(('dp', 'ep'))
- w_router: bfloat16 [1024, 8], replicated
- w_in: bfloat16 [8, 1024, 4096], P('ep', None, 'tp')
- w_out: bfloat16 [8, 4096, 1024], P('ep', 'tp')
- expert_ids: int32 [1024], P(('dp', 'ep'))
Outputs:
- output 1: bfloat16 [1024, 1024], P(('dp', 'ep'))
- output 2: bfloat16 [1024, 1024], P(('dp', 'ep'))
- output 3: float32 [8, 1024, 4096], P(('dp', 'ep'), None, 'tp')
- output 4: float32 [8, 4096, 1024], P(('dp', 'ep'), 'tp')
- output 5: float32 [1024, 8], P('dp')
All inputs are finite; a program needn't handle non-finite values.
Results may differ from a plain program's by a relative error of at most 0.00633399.
Values are sent between devices in bfloat16 or wider.
A program may use at most 1 GiB of HBM per device.

v0:
```python
import jax
import jax.numpy as jnp
from jax import lax
from jax.sharding import PartitionSpec as P


def solution(mesh):
    ep_size = mesh.shape["ep"]
    row_spec = P(("dp", "ep"), None)

    def local_block(tokens, grad_out, w_router, w_in, w_out, expert_ids):
        n_local, d_model = tokens.shape
        n_experts = w_router.shape[1]
        local_experts = w_in.shape[0]
        capacity = (6 * n_local + 5 * n_experts - 1) // (5 * n_experts)
        n_slots = n_experts * capacity
        chosen = expert_ids[:, None] == jnp.arange(n_experts)[None, :]
        one_hot = chosen.astype(jnp.int32)
        position = jnp.sum(jnp.cumsum(one_hot, axis=0) * one_hot, axis=1) - 1
        slot_index = jnp.where(position < capacity, expert_ids * capacity + position, n_slots)

        def dispatch(rows):
            slot_buf = jnp.zeros((n_slots + 1, d_model), rows.dtype).at[slot_index].set(rows)
            send_buf = slot_buf[:n_slots].reshape(ep_size, local_experts, capacity, d_model)
            recv_buf = lax.all_to_all(send_buf, "ep", 0, 2, tiled=True)
            return recv_buf.reshape(local_experts, ep_size * capacity, d_model)

        def combine(expert_rows):
            send_buf = expert_rows.reshape(local_experts, ep_size, capacity, d_model)
            recv_buf = lax.all_to_all(send_buf, "ep", 1, 0, tiled=True)
            padded = jnp.concatenate([recv_buf.reshape(n_slots, d_model), jnp.zeros((1, d_model), expert_rows.dtype)], axis=0)
            return jnp.take(padded, slot_index, axis=0)

        logits = jnp.dot(tokens, w_router, preferred_element_type=jnp.float32)
        router_prob = jax.nn.softmax(logits, axis=-1)
        gate_prob = jnp.sum(jnp.where(chosen, router_prob, 0.0), axis=1)

        slot_rows = dispatch(tokens)
        pre_act = jnp.einsum("erd,edf->erf", slot_rows, w_in, preferred_element_type=jnp.float32)
        act_val, act_vjp = jax.vjp(jax.nn.gelu, pre_act)
        hidden = act_val.astype(jnp.bfloat16)
        y_part = jnp.einsum("erf,efd->erd", hidden, w_out, preferred_element_type=jnp.float32)
        y_rows = lax.psum(y_part, "tp").astype(jnp.bfloat16)
        y_tok = combine(y_rows)
        moe_out = (gate_prob[:, None] * y_tok.astype(jnp.float32)).astype(jnp.bfloat16)

        dy_tok = (gate_prob[:, None] * grad_out.astype(jnp.float32)).astype(jnp.bfloat16)
        dy_rows = dispatch(dy_tok)
        d_hidden = jnp.einsum("erd,efd->erf", dy_rows, w_out, preferred_element_type=jnp.float32)
        d_pre = act_vjp(d_hidden)[0].astype(jnp.bfloat16)
        grad_w_out = jnp.einsum("erf,erd->efd", hidden, dy_rows, preferred_element_type=jnp.float32)
        grad_w_in = jnp.einsum("erd,erf->edf", slot_rows, d_pre, preferred_element_type=jnp.float32)
        d_part = jnp.einsum("erf,edf->erd", d_pre, w_in, preferred_element_type=jnp.float32)
        d_slot = lax.psum(d_part, "tp").astype(jnp.bfloat16)
        dx_moe = combine(d_slot)

        d_gate = jnp.sum(grad_out.astype(jnp.float32) * y_tok.astype(jnp.float32), axis=1)
        d_logits = (d_gate[:, None] * router_prob * (chosen.astype(jnp.float32) - gate_prob[:, None])).astype(jnp.bfloat16)
        router_grad = jnp.einsum("te,de->td", d_logits, w_router, preferred_element_type=jnp.float32)
        grad_tokens = (dx_moe.astype(jnp.float32) + router_grad).astype(jnp.bfloat16)
        grad_w_router = lax.psum(jnp.einsum("td,te->de", tokens, d_logits, preferred_element_type=jnp.float32), "ep")
        return moe_out, grad_tokens, grad_w_in, grad_w_out, grad_w_router

    in_specs = (row_spec, row_spec, P(None, None), P("ep", None, "tp"), P("ep", "tp", None), P(("dp", "ep")))
    out_specs = (row_spec, row_spec, P(("dp", "ep"), None, "tp"), P(("dp", "ep"), "tp", None), P("dp", None))
    return jax.shard_map(local_block, mesh=mesh, in_specs=in_specs, out_specs=out_specs, check_vma=False)
```

profile of v0, /device:TPU:0, one launch (start us, length us, event | category | flops | bytes accessed | tf_op | source)
XLA Modules:
  0.0 167.9 jit_solution(6768264904878782295)
XLA Ops:
  0.6 0.7 fusion.28
  1.3 0.6 reduce-window.6
  1.9 0.2 slice_reduce_fusion
  2.2 0.8 fusion.27
  2.9 0.7 compare_and_fusion
  3.6 2.4 %scatter_custom_fusion = bf16[313,1024]{1,0:T(8,128)(2,1)S(1)} fusion(s32[256]{0:T(256)S(1)} %get-tuple-element.9, bf16[256,1024]{1,0:T(8,128)(2,1)} %param.8, bf16[]{:T(256)} %constant.6.clone.1), kind=kCustom, calls=%fused_computation.35 | custom fusion | bytes 641536 | tf_op jit(solution)/shard_map/scatter | solution.py:23
  6.1 0.2 reshape.64
  6.3 1.5 copy.17
  7.8 4.6 %all-to-all-start = ((bf16[4,2,39,1024]{3,1,2,0:T(2,128)(2,1)}), bf16[4,2,39,1024]{3,1,2,0:T(2,128)(2,1)S(1)}, u32[]{:S(2)}, u32[]{:S(2)}) async-start(bf16[4,2,39,1024]{3,1,2,0:T(2,128)(2,1)} %copy.17), calls=%async_computation | async-start | bytes 1277952 | tf_op jit(solution)/shard_map/all_to_all | solution.py:25
  12.4 0.3 fusion.32
  12.7 1.9 %scatter_custom_fusion.1 = bf16[313,1024]{1,0:T(8,128)(2,1)S(1)} fusion(s32[256]{0:T(256)S(1)} %get-tuple-element.9, bf16[256,1024]{1,0:T(8,128)(2,1)S(1)} %copy-done.3, f32[256]{0:T(256)S(1)} %select_reduce_fusion, bf16[]{:T(256)} %constant.6.clone.1), kind=kCustom, calls=%fused_computation.31 | custom fusion | flops 786432 | bytes 1166338 | tf_op jit(solution)/shard_map/scatter | solution.py:23
  14.9 1.5 copy.21
  16.4 5.8 %all-to-all-done = bf16[4,2,39,1024]{3,1,2,0:T(2,128)(2,1)S(1)} async-done(((bf16[4,2,39,1024]{3,1,2,0:T(2,128)(2,1)}), bf16[4,2,39,1024]{3,1,2,0:T(2,128)(2,1)S(1)}, u32[]{:S(2)}, u32[]{:S(2)}) %all-to-all-start) | async-done | bytes 639008 | tf_op jit(solution)/shard_map/all_to_all | solution.py:25
  22.2 4.3 %all-to-all-start.2 = ((bf16[4,2,39,1024]{3,1,2,0:T(2,128)(2,1)}), bf16[4,2,39,1024]{3,1,2,0:T(2,128)(2,1)}, u32[]{:S(2)}, u32[]{:S(2)}) async-start(bf16[4,2,39,1024]{3,1,2,0:T(2,128)(2,1)} %copy.21), calls=%async_computation.2 | async-start | bytes 1277952 | tf_op jit(solution)/shard_map/all_to_all | solution.py:25
  26.6 4.9 %fusion.19 = f32[2,156,2048]{2,1,0:T(8,128)S(1)} fusion(bf16[2,1024,2048]{2,1,0:T(8,128)(2,1)} %param.11, bf16[2,156,1024]{2,0,1:T(2,128)(2,1)S(1)} %bitcast.43), kind=kOutput, calls=%fused_computation.29 | convolution fusion | flops 1308622848 | bytes 11583488 | tf_op jit(solution)/shard_map/erd,edf->erf/dot_general | solution.py:39
  31.5 6.3 %fusion.31 = f32[2,156,1024]{2,1,0:T(8,128)} fusion(bf16[2,2048,1024]{2,1,0:T(8,128)(2,1)} %param.12, f32[2,156,2048]{2,1,0:T(8,128)S(1)} %fusion.19), kind=kOutput, calls=%fused_computation.52 | convolution fusion | flops 1314373632 | bytes 12222464 | tf_op jit(solution)/shard_map/erf,efd->erd/dot_general | solution.py:42
  37.9 7.5 %fusion.6 = bf16[2,156,2048]{2,1,0:T(8,128)(2,1)S(1)} fusion(f32[2,156,2048]{2,1,0:T(8,128)S(1)} %fusion.19, bf16[2,2048,1024]{2,1,0:T(8,128)(2,1)} %param.12, bf16[2,156,1024]{2,0,1:T(2,128)(2,1)} %bitcast.11), kind=kOutput, calls=%fused_computation.12 | convolution fusion | flops 1321402368 | bytes 12861440 | tf_op jit(solution)/shard_map/erd,efd->erf/dot_general | solution.py:49
  45.4 10.2 %fusion.11 = f32[2,2048,1024]{2,1,0:T(8,128)} fusion(bf16[2,156,1024]{2,0,1:T(2,128)(2,1)} %bitcast.11, f32[2,156,2048]{2,1,0:T(8,128)S(1)} %fusion.19), kind=kOutput, calls=%fused_computation.23 | convolution fusion | flops 1314373632 | bytes 19972096 | tf_op jit(solution)/shard_map/erf,erd->efd/dot_general | solution.py:51
  55.6 6.3 %fusion.33 = f32[2,156,1024]{2,1,0:T(8,128)S(1)} fusion(bf16[2,156,2048]{2,1,0:T(8,128)(2,1)S(1)} %fusion.6, bf16[2,1024,2048]{2,1,0:T(8,128)(2,1)} %param.11), kind=kOutput, calls=%fused_computation.54 | convolution fusion | flops 1308622848 | bytes 10944512 | tf_op jit(solution)/shard_map/erf,edf->erd/dot_general | solution.py:53
  61.9 66.9 %all-reduce.4 = (bf16[2,156,1024]{2,1,0:T(8,128)(2,1)}, bf16[2,156,1024]{2,1,0:T(8,128)(2,1)}) all-reduce(f32[2,156,1024]{2,1,0:T(8,128)} %fusion.31, f32[2,156,1024]{2,1,0:T(8,128)S(1)} %fusion.33), channel_id=1, replica_groups=mesh['dp'=1,'tp'=2,'ep'=4] {'tp'}, use_global_device_ids=true, to_apply=%region_7.8 | all-reduce | flops 638976 | bytes 3833856 | tf_op jit(solution)/shard_map/psum | solution.py:43
  128.9 2.7 %copy.26 = bf16[2,156,1024]{2,0,1:T(2,128)(2,1)} copy(bf16[2,156,1024]{2,1,0:T(8,128)(2,1)} %get-tuple-element.6) | data formatting | bytes 1277952 | tf_op jit(solution)/shard_map/reshape | solution.py:29
  131.5 3.7 %all-to-all-start.1 = ((bf16[2,4,39,1024]{3,0,2,1:T(2,128)(2,1)}), bf16[2,4,39,1024]{3,0,2,1:T(2,128)(2,1)S(1)}, u32[]{:S(2)}, u32[]{:S(2)}) async-start(bf16[2,4,39,1024]{3,0,2,1:T(2,128)(2,1)} %bitcast.6), calls=%async_computation.1 | async-start | bytes 1277952 | tf_op jit(solution)/shard_map/all_to_all | solution.py:30
  135.2 1.5 copy.28
  136.7 8.6 %fusion.17 = f32[2,1024,2048]{2,1,0:T(8,128)} fusion(bf16[2,156,2048]{2,1,0:T(8,128)(2,1)S(1)} %copy-done.2, bf16[2,156,1024]{2,0,1:T(2,128)(2,1)S(1)} %bitcast.44), kind=kOutput, calls=%fused_computation.27 | convolution fusion | flops 1308622848 | bytes 18694144 | tf_op jit(solution)/shard_map/erd,erf->edf/dot_general | solution.py:52
  145.4 3.5 %all-to-all-start.3 = ((bf16[2,4,39,1024]{3,0,2,1:T(2,128)(2,1)}), bf16[2,4,39,1024]{3,0,2,1:T(2,128)(2,1)S(1)}, u32[]{:S(2)}, u32[]{:S(2)}) async-start(bf16[2,4,39,1024]{3,0,2,1:T(2,128)(2,1)} %bitcast.12), calls=%async_computation.3 | async-start | bytes 1277952 | tf_op jit(solution)/shard_map/all_to_all | solution.py:30
  149.0 0.2 reshape.67
  149.3 1.2 gather_fusion
  150.5 1.2 fusion.10
  151.9 13.3 %psum.23 = f32[1024,8]{0,1:T(8,128)} all-reduce(f32[1024,8]{0,1:T(8,128)S(1)} %convolution_bitcast_fusion), channel_id=1, replica_groups=mesh['dp'=1,'tp'=2,'ep'=4] {'ep'}, use_global_device_ids=true, to_apply=%region_11.13 | all-reduce | flops 8192 | bytes 65536 | tf_op jit(solution)/shard_map/psum | solution.py:61
  165.3 0.2 reshape.71
  165.6 1.2 gather_fusion.1
  166.8 1.1 fusion.7
  (34 shorter events, 1.0 us)
Async XLA Ops:
  0.6 11.8 %copy-start = (bf16[1024,8]{0,1:T(8,128)(2,1)S(1)}, bf16[1024,8]{0,1:T(8,128)(2,1)}, u32[]{:S(2)}) copy-start(bf16[1024,8]{0,1:T(8,128)(2,1)} %param.10) | copy-start | bytes 49156
  6.0 6.4 %copy-start.5 = (bf16[256,1024]{1,0:T(8,128)(2,1)S(1)}, bf16[256,1024]{1,0:T(8,128)(2,1)}, u32[]{:S(2)}) copy-start(bf16[256,1024]{1,0:T(8,128)(2,1)} %param.8) | copy-start | bytes 1572868
  6.0 6.7 %copy-start.8 = (s32[256]{0:T(256)S(1)}, s32[256]{0:T(256)}, u32[]{:S(2)}) copy-start(s32[256]{0:T(256)} %param.13) | copy-start | bytes 3076
  6.0 6.7 %copy-start.3 = (bf16[256,1024]{1,0:T(8,128)(2,1)S(1)}, bf16[256,1024]{1,0:T(8,128)(2,1)}, u32[]{:S(2)}) copy-start(bf16[256,1024]{1,0:T(8,128)(2,1)} %param.9) | copy-start | bytes 1572868
  7.8 14.4 %all-to-all-start = ((bf16[4,2,39,1024]{3,1,2,0:T(2,128)(2,1)}), bf16[4,2,39,1024]{3,1,2,0:T(2,128)(2,1)S(1)}, u32[]{:S(2)}, u32[]{:S(2)}) async-start(bf16[4,2,39,1024]{3,1,2,0:T(2,128)(2,1)} %copy.17), calls=%async_computation | async-start | bytes 1277952 | tf_op jit(solution)/shard_map/all_to_all | solution.py:25
  22.2 15.6 %all-to-all-start.2 = ((bf16[4,2,39,1024]{3,1,2,0:T(2,128)(2,1)}), bf16[4,2,39,1024]{3,1,2,0:T(2,128)(2,1)}, u32[]{:S(2)}, u32[]{:S(2)}) async-start(bf16[4,2,39,1024]{3,1,2,0:T(2,128)(2,1)} %copy.21), calls=%async_computation.2 | async-start | bytes 1277952 | tf_op jit(solution)/shard_map/all_to_all | solution.py:25
  45.4 10.2 %copy-start.1 = (bf16[2,156,2048]{2,1,0:T(8,128)(2,1)}, bf16[2,156,2048]{2,1,0:T(8,128)(2,1)S(1)}, u32[]{:S(2)}) copy-start(bf16[2,156,2048]{2,1,0:T(8,128)(2,1)S(1)} %fusion.6) | copy-start | bytes 3833860
  61.9 74.8 %copy-start.2 = (bf16[2,156,2048]{2,1,0:T(8,128)(2,1)S(1)}, bf16[2,156,2048]{2,1,0:T(8,128)(2,1)}, u32[]{:S(2)}) copy-start(bf16[2,156,2048]{2,1,0:T(8,128)(2,1)} %copy-done.1) | copy-start | bytes 3833860
  128.9 6.4 %copy-start.7 = (bf16[2,156,1024]{2,1,0:T(8,128)(2,1)S(1)}, bf16[2,156,1024]{2,1,0:T(8,128)(2,1)}, u32[]{:S(2)}) copy-start(bf16[2,156,1024]{2,1,0:T(8,128)(2,1)} %get-tuple-element.7) | copy-start | bytes 1916932
  131.5 13.9 %all-to-all-start.1 = ((bf16[2,4,39,1024]{3,0,2,1:T(2,128)(2,1)}), bf16[2,4,39,1024]{3,0,2,1:T(2,128)(2,1)S(1)}, u32[]{:S(2)}, u32[]{:S(2)}) async-start(bf16[2,4,39,1024]{3,0,2,1:T(2,128)(2,1)} %bitcast.6), calls=%async_computation.1 | async-start | bytes 1277952 | tf_op jit(solution)/shard_map/all_to_all | solution.py:30
  145.4 19.8 %all-to-all-start.3 = ((bf16[2,4,39,1024]{3,0,2,1:T(2,128)(2,1)}), bf16[2,4,39,1024]{3,0,2,1:T(2,128)(2,1)S(1)}, u32[]{:S(2)}, u32[]{:S(2)}) async-start(bf16[2,4,39,1024]{3,0,2,1:T(2,128)(2,1)} %bitcast.12), calls=%async_computation.3 | async-start | bytes 1277952 | tf_op jit(solution)/shard_map/all_to_all | solution.py:30
  149.3 1.2 copy-start.4
  149.3 2.4 %copy-start.6 = (bf16[256,1024]{1,0:T(8,128)(2,1)S(1)}, bf16[256,1024]{1,0:T(8,128)(2,1)}, u32[]{:S(2)}) copy-start(bf16[256,1024]{1,0:T(8,128)(2,1)} %param.8) | copy-start | bytes 1572868
where the time goes:
time: 169 us; the launch traced here: 168 us
  blocking collectives  80.2 us (47%)
  matrix products  45.5 us (27%)
  starting transfers between devices  16.1 us (10%)
  local copies, waits for them, and re-layouts  13.4 us (8%)
  other arithmetic  5.9 us (3%)
  waiting for transfers between devices  5.81 us (3%)
    psum x1, blocking collectives, local_block(): y_rows = lax.psum(y_part, 'tp').astype(jnp.bfloat16)  66.9 us
    psum x1, blocking collectives, local_block(): lax.psum(jnp.einsum('td,te->de', tokens, d_logits, preferred_element_type...  13.3 us
    dot_general x1, matrix products, local_block(): jnp.einsum('erf,erd->efd', hidden, dy_rows, preferred_element_type=jnp.fl...  10.2 us
    all_to_all x2, starting transfers between devices, dispatch(): recv_buf = lax.all_to_all(send_buf, 'ep', 0, 2, tiled=True)  8.95 us
    dot_general x1, matrix products, local_block(): jnp.einsum('erd,erf->edf', slot_rows, d_pre, preferred_element_type=jnp.f...  8.63 us
    dot_general x1, matrix products, local_block(): jnp.einsum('erd,efd->erf', dy_rows, w_out, preferred_element_type=jnp.flo...  7.52 us
    all_to_all x2, starting transfers between devices, combine(): recv_buf = lax.all_to_all(send_buf, 'ep', 1, 0, tiled=True)  7.18 us
    dot_general x1, matrix products, local_block(): jnp.einsum('erf,efd->erd', hidden, w_out, preferred_element_type=jnp.floa...  6.34 us
  transfers between devices with their start and end apart: 4, of which 1 were waited for; matrix products, arithmetic and copies ran while one was open for 17% of the time, Pallas kernels for 0%

commit v1 on v0

v1 whole, which is shorter than its diff:
```python
import jax
import jax.numpy as jnp
from jax import lax
from jax.experimental import pallas as pl
from jax.experimental.pallas import tpu as pltpu
from jax.sharding import PartitionSpec as P

MESH = pl.DeviceIdType.MESH
F32, BF16 = jnp.float32, jnp.bfloat16
CONTRACT_LAST = (((1,), (1,)), ((), ()))
CONTRACT_FIRST = (((0,), (0,)), ((), ()))
GELU_C = 0.7978845608028654
GELU_K = 0.044715


def mm(a, b, dims=(((1,), (0,)), ((), ()))):
    return lax.dot_general(a, b, dims, preferred_element_type=F32)


def ep_partners():
    ep = lax.axis_index("ep")
    cx, cc = ep // 2, ep % 2
    return [ep, 2 * cx + (1 - cc), 2 * (1 - cx) + cc, 2 * (1 - cx) + (1 - cc)]


def route(idx_row, capacity, n_experts, stride):
    n = idx_row.shape[1]
    expert = lax.broadcasted_iota(jnp.int32, (n_experts, n), 0)
    hot = jnp.where(expert == idx_row, 1.0, 0.0)
    earlier = lax.broadcasted_iota(jnp.int32, (n, n), 0)
    later = lax.broadcasted_iota(jnp.int32, (n, n), 1)
    upto = jnp.where(earlier <= later, 1.0, 0.0).astype(BF16)
    count = mm(hot.astype(BF16), upto)
    position = jnp.sum(hot * count, axis=0, keepdims=True) - 1.0
    slot = jnp.where(position < capacity, idx_row.astype(F32) * stride + position, -1.0)
    return hot, slot


def pick(slot, first, rows):
    n = slot.shape[1]
    row = (lax.broadcasted_iota(jnp.int32, (rows, n), 0) + first).astype(F32)
    return jnp.where(row == slot, 1.0, 0.0).astype(BF16)


def gate_of(x, wgt, hot):
    n_experts = hot.shape[0]
    logits = mm(x, wgt, CONTRACT_LAST)
    e = jnp.exp(logits - jnp.max(logits, axis=1, keepdims=True))
    prob = e / jnp.sum(e, axis=1, keepdims=True)
    eye = jnp.where(
        lax.broadcasted_iota(jnp.int32, (n_experts, n_experts), 0)
        == lax.broadcasted_iota(jnp.int32, (n_experts, n_experts), 1), 1.0, 0.0)
    chosen = mm(hot.astype(BF16), eye.astype(BF16), CONTRACT_FIRST)
    gate = jnp.sum(chosen * prob, axis=1, keepdims=True)
    return prob, chosen, gate


def enter(peers, tp_peer):
    barrier = pltpu.get_barrier_semaphore()
    for r in (1, 2, 3):
        pl.semaphore_signal(barrier, inc=1, device_id={"ep": peers[r]}, device_id_type=MESH)
    pl.semaphore_signal(barrier, inc=1, device_id={"tp": tp_peer}, device_id_type=MESH)
    return barrier


def send(src, dst, ssem, rsem, device):
    copy = pltpu.make_async_remote_copy(
        src_ref=src, dst_ref=dst, send_sem=ssem, recv_sem=rsem, device_id=device, device_id_type=MESH)
    copy.start()
    return copy


def pair(lo, hi, e, cap):
    a = lo.astype(F32)[e * cap:(e + 1) * cap]
    b = hi.astype(F32)[e * cap:(e + 1) * cap]
    return jnp.concatenate([a, b], axis=0).astype(BF16)


def make_front(n_experts, capacity, cap):
    blk = 2 * cap

    def front(x_ref, gy_ref, wgt_ref, idx_ref, wi_hbm, wo_hbm,
              h_ref, da_ref, xs_ref, dys_ref, speer_ref, sown_ref, yr_ref,
              wi, wo, xsend, dysend, xrecv, dyrecv, gp, ypeer, yown, yrecv, yback, yland,
              wsem, x_s, x_r, d_s, d_r, y_s, y_r, b_s, b_r):
        tp = lax.axis_index("tp")
        tp_peer = 1 - tp
        peers = ep_partners()
        half = x_ref.shape[1] // 2
        d_ff = wi.shape[2]
        loads = {}
        for e in range(2):
            loads["i", e] = pltpu.make_async_copy(wi_hbm.at[e], wi.at[e], wsem.at[0, e])
            loads["o", e] = pltpu.make_async_copy(wo_hbm.at[e], wo.at[e], wsem.at[1, e])
        for e in range(2):
            loads["i", e].start()
            loads["o", e].start()
        barrier = enter(peers, tp_peer)

        x = x_ref[...]
        hot, slot = route(idx_ref[...], capacity, n_experts, cap)
        picks = [pick(slot, peers[r] * blk, blk) for r in range(4)]
        for r in (2, 3, 1, 0):
            xsend[r] = mm(picks[r], x).astype(BF16)
        pl.semaphore_wait(barrier, 4)
        sends = []
        xc, dc = {}, {}
        for r in (2, 3, 1):
            xc[r] = send(xsend.at[r], xrecv.at[r - 1], x_s.at[r - 1], x_r.at[r - 1], {"ep": peers[r]})
        _, _, gate = gate_of(x, wgt_ref[...], hot)
        dy = (gate * gy_ref[...].astype(F32)).astype(BF16)
        for r in (2, 3, 1, 0):
            dysend[r] = mm(picks[r], dy).astype(BF16)
            if r:
                dc[r] = send(dysend.at[r], dyrecv.at[r - 1], d_s.at[r - 1], d_r.at[r - 1], {"ep": peers[r]})

        yc = {}

        def forward(g):
            rows = slice(g * blk, (g + 1) * blk)
            for e in range(2):
                lo = xsend[0] if g == 0 else xrecv[1]
                hi = xrecv[0] if g == 0 else xrecv[2]
                xs_ref[e, rows, :] = pair(lo, hi, e, cap)
            for e in range(2):
                if g == 0:
                    loads["i", e].wait()
                xg = xs_ref[e, rows, :]
                step = d_ff // 2
                for c in range(2):
                    cols = slice(c * step, (c + 1) * step)
                    a = mm(xg, wi[e, :, cols])
                    t = jnp.tanh(GELU_C * (a + GELU_K * (a * a * a)))
                    cdf = 0.5 * (1.0 + t)
                    h_ref[e, rows, cols] = (a * cdf).astype(BF16)
                    gp[e, rows, cols] = cdf + (0.5 * a) * (1.0 - t * t) * (GELU_C + (3.0 * GELU_C * GELU_K) * (a * a))
                if g == 0:
                    loads["o", e].wait()
                hg = h_ref[e, rows, :]
                ypeer[g, e] = mm(hg, wo[e, :, pl.ds(pl.multiple_of(tp_peer * half, half), half)])
                yc[g, e] = send(ypeer.at[g, e], yrecv.at[g, e], y_s.at[g, e], y_r.at[g, e], {"tp": tp_peer})
                yown[g, e] = mm(hg, wo[e, :, pl.ds(pl.multiple_of(tp * half, half), half)])

        def backward(e):
            for g in range(2):
                lo = dysend[0] if g == 0 else dyrecv[1]
                hi = dyrecv[0] if g == 0 else dyrecv[2]
                dys_ref[e, g * blk:(g + 1) * blk, :] = pair(lo, hi, e, cap)
            dyg = dys_ref[e]
            step = d_ff // 4
            for c in range(4):
                cols = slice(c * step, (c + 1) * step)
                dh = mm(dyg, wo[e, cols, :], CONTRACT_LAST)
                da_ref[e, :, cols] = (dh * gp[e, :, cols]).astype(BF16)
            dag = da_ref[e]
            speer_ref[e] = mm(dag, wi[e, pl.ds(pl.multiple_of(tp_peer * half, half), half), :], CONTRACT_LAST)
            sown_ref[e] = mm(dag, wi[e, pl.ds(pl.multiple_of(tp * half, half), half), :], CONTRACT_LAST)

        bc = {}

        def give_back(g):
            for e in range(2):
                yc[g, e].wait()
            both = [yown[g, e] + yrecv[g, e] for e in range(2)]
            for q in range(2):
                r = 2 * g + q
                block = jnp.concatenate([both[e][q * cap:(q + 1) * cap] for e in range(2)], axis=0).astype(BF16)
                if r == 0:
                    yr_ref[0] = block
                else:
                    yback[r - 1] = block
                    bc[r] = send(yback.at[r - 1], yland.at[r - 1], b_s.at[r - 1], b_r.at[r - 1], {"ep": peers[r]})

        xc[1].wait()
        forward(0)
        xc[2].wait()
        xc[3].wait()
        forward(1)
        for r in (1, 2, 3):
            dc[r].wait()
        backward(0)
        give_back(0)
        backward(1)
        give_back(1)
        for r in (1, 2, 3):
            bc[r].wait()
            yr_ref[r] = yland[r - 1]

    return front


def grads_kernel(h_ref, dys_ref, xs_ref, da_ref, dwi_ref, dwo_ref):
    dwo_ref[0] = mm(h_ref[0], dys_ref[0], CONTRACT_FIRST)
    dwi_ref[0] = mm(xs_ref[0], da_ref[0], CONTRACT_FIRST)


def make_back(n_experts, capacity, cap):
    blk = 2 * cap

    def back(x_ref, gy_ref, wgt_ref, idx_ref, yr_ref, sown_ref, srecv_ref,
             out_ref, dx_ref, dwgt_ref,
             ysend, yland, sback, sland, dxsend, dxland, dwg,
             y_s, y_r, b_s, b_r, x_s, x_r, w_s, w_r):
        tp = lax.axis_index("tp")
        ep = lax.axis_index("ep")
        tp_peer = 1 - tp
        peers = ep_partners()
        half = x_ref.shape[1] // 2
        mine = pl.ds(pl.multiple_of(tp * half, half), half)
        theirs = pl.ds(pl.multiple_of(tp_peer * half, half), half)
        barrier = enter(peers, tp_peer)
        hot, slot = route(idx_ref[...], capacity, n_experts, cap)
        picks = jnp.concatenate([pick(slot, peers[r] * blk, blk) for r in range(4)], axis=0)
        ysend[...] = mm(picks, yr_ref[...], CONTRACT_FIRST).astype(BF16)
        pl.semaphore_wait(barrier, 4)
        yc = send(ysend, yland, y_s, y_r, {"tp": tp_peer})

        bc = {}
        for g in (1, 0):
            rows = slice(g * blk, (g + 1) * blk)
            both = [sown_ref[e, rows, :] + srecv_ref[e, rows, :] for e in range(2)]
            for q in range(2):
                r = 2 * g + q
                block = jnp.concatenate([both[e][q * cap:(q + 1) * cap] for e in range(2)], axis=0).astype(BF16)
                if r == 0:
                    sland[0:blk, :] = block
                else:
                    sback[r - 1] = block
                    bc[r] = send(sback.at[r - 1], sland.at[r * blk:(r + 1) * blk, :], b_s.at[r - 1], b_r.at[r - 1],
                                 {"ep": peers[r]})

        x = x_ref[...]
        prob, chosen, gate = gate_of(x, wgt_ref[...], hot)
        y_mine = ysend[...].astype(F32)
        out_ref[:, mine] = (gate * y_mine).astype(BF16)
        dgate = jnp.sum(gy_ref[:, mine].astype(F32) * y_mine, axis=1, keepdims=True)
        yc.wait()
        y_theirs = yland[...].astype(F32)
        out_ref[:, theirs] = (gate * y_theirs).astype(BF16)
        dgate = dgate + jnp.sum(gy_ref[:, theirs].astype(F32) * y_theirs, axis=1, keepdims=True)
        dlogits = (dgate * prob * (chosen - gate)).astype(BF16)
        dwg[ep] = mm(dlogits, x, CONTRACT_FIRST)
        wc = {}
        for r in (2, 3, 1):
            wc[r] = send(dwg.at[ep], dwg.at[ep], w_s.at[r - 1], w_r.at[r - 1], {"ep": peers[r]})
        rgrad = mm(dlogits, wgt_ref[:, mine])
        for r in (1, 2, 3):
            bc[r].wait()
        s_tok = mm(picks, sland[...], CONTRACT_FIRST).astype(BF16).astype(F32)
        dx_mine = (s_tok + rgrad).astype(BF16)
        dxsend[...] = dx_mine
        xc = send(dxsend, dxland, x_s, x_r, {"tp": tp_peer})
        dx_ref[:, mine] = dx_mine
        for r in (1, 2, 3):
            wc[r].wait()
        dwgt_ref[...] = (dwg[0] + dwg[1]) + (dwg[2] + dwg[3])
        xc.wait()
        dx_ref[:, theirs] = dxland[...]

    return back


def solution(mesh):
    row_spec = P(("dp", "ep"), None)
    vmem = pl.BlockSpec(memory_space=pltpu.VMEM)
    hbm = pl.BlockSpec(memory_space=pl.ANY)

    def local_block(tokens, grad_out, w_router, w_in, w_out, expert_ids):
        n, d_model = tokens.shape
        n_experts = w_router.shape[1]
        le, _, d_ff = w_in.shape
        capacity = (6 * n + 5 * n_experts - 1) // (5 * n_experts)
        cap = -(-capacity // 8) * 8
        blk = le * cap
        rows = 4 * cap
        half = d_model // 2
        wgt = w_router.T
        idx_row = expert_ids.reshape(1, n)
        sds = jax.ShapeDtypeStruct
        dma = pltpu.SemaphoreType.DMA

        h, da, xs, dys, speer, sown, yr = pl.pallas_call(
            make_front(n_experts, capacity, cap),
            out_shape=(sds((le, rows, d_ff), BF16), sds((le, rows, d_ff), BF16), sds((le, rows, d_model), BF16),
                       sds((le, rows, d_model), BF16), sds((le, rows, half), F32), sds((le, rows, half), F32),
                       sds((4, blk, half), BF16)),
            in_specs=[vmem, vmem, vmem, vmem, hbm, hbm],
            out_specs=(vmem,) * 7,
            scratch_shapes=[
                pltpu.VMEM((le, d_model, d_ff), BF16), pltpu.VMEM((le, d_ff, d_model), BF16),
                pltpu.VMEM((4, blk, d_model), BF16), pltpu.VMEM((4, blk, d_model), BF16),
                pltpu.VMEM((3, blk, d_model), BF16), pltpu.VMEM((3, blk, d_model), BF16),
                pltpu.VMEM((le, rows, d_ff), F32),
                pltpu.VMEM((2, le, blk, half), F32), pltpu.VMEM((2, le, blk, half), F32), pltpu.VMEM((2, le, blk, half), F32),
                pltpu.VMEM((3, blk, half), BF16), pltpu.VMEM((3, blk, half), BF16),
                dma((2, le)), dma((3,)), dma((3,)), dma((3,)), dma((3,)), dma((2, le)), dma((2, le)), dma((3,)), dma((3,)),
            ],
            compiler_params=pltpu.CompilerParams(collective_id=0, has_side_effects=True, vmem_limit_bytes=48 * 2**20),
            name="front",
        )(tokens, grad_out, wgt, idx_row, w_in, w_out)

        srecv = lax.ppermute(speer, "tp", [(0, 1), (1, 0)])

        steps = 4
        hs, ms = d_ff // steps, d_model // steps
        dwi, dwo = pl.pallas_call(
            grads_kernel,
            grid=(le, steps),
            out_shape=(sds((le, d_model, d_ff), F32), sds((le, d_ff, d_model), F32)),
            in_specs=[pl.BlockSpec((1, rows, hs), lambda e, c: (e, 0, c)), pl.BlockSpec((1, rows, d_model), lambda e, c: (e, 0, 0)),
                      pl.BlockSpec((1, rows, ms), lambda e, c: (e, 0, c)), pl.BlockSpec((1, rows, d_ff), lambda e, c: (e, 0, 0))],
            out_specs=(pl.BlockSpec((1, ms, d_ff), lambda e, c: (e, c, 0)), pl.BlockSpec((1, hs, d_model), lambda e, c: (e, c, 0))),
            cost_estimate=pl.CostEstimate(flops=4 * le * rows * d_model * d_ff, bytes_accessed=8 * le * d_model * d_ff,
                                          transcendentals=0),
            compiler_params=pltpu.CompilerParams(vmem_limit_bytes=24 * 2**20),
            name="weight_grads",
        )(h, dys, xs, da)

        out, dx, dwgt = pl.pallas_call(
            make_back(n_experts, capacity, cap),
            out_shape=(sds((n, d_model), BF16), sds((n, d_model), BF16), sds((n_experts, d_model), F32)),
            in_specs=[vmem] * 7,
            out_specs=(vmem,) * 3,
            scratch_shapes=[
                pltpu.VMEM((n, half), BF16), pltpu.VMEM((n, half), BF16),
                pltpu.VMEM((3, blk, half), BF16), pltpu.VMEM((4 * blk, half), BF16),
                pltpu.VMEM((n, half), BF16), pltpu.VMEM((n, half), BF16),
                pltpu.VMEM((4, n_experts, d_model), F32),
                dma, dma, dma((3,)), dma((3,)), dma, dma, dma((3,)), dma((3,)),
            ],
            compiler_params=pltpu.CompilerParams(collective_id=1, has_side_effects=True, vmem_limit_bytes=24 * 2**20),
            name="back",
        )(tokens, grad_out, wgt, idx_row, yr.reshape(4 * blk, half), sown, srecv)
        return out, dx, dwi, dwo, dwgt.T

    in_specs = (row_spec, row_spec, P(None, None), P("ep", None, "tp"), P("ep", "tp", None), P(("dp", "ep")))
    out_specs = (row_spec, row_spec, P(("dp", "ep"), None, "tp"), P(("dp", "ep"), "tp", None), P("dp", None))
    return jax.shard_map(local_block, mesh=mesh, in_specs=in_specs, out_specs=out_specs, check_vma=False)
```

time: 169 us -> 70.6 us (0.42)
  blocking collectives: 80.2 us -> 0 us
  Pallas kernels: 0 us -> 58.7 us
  matrix products: 45.5 us -> 0 us
  starting transfers between devices: 16.1 us -> 1.56 us
  local copies, waits for them, and re-layouts: 13.4 us -> 7 us
  other arithmetic: 5.9 us -> 0 us
  waiting for transfers between devices: 5.81 us -> 2.4 us
    psum x2 -> x0, blocking collectives: 80.2 us -> none  [the longest x1 66.9 us: local_block(): y_rows = lax.psum(y_part, 'tp').astype(jnp.bfloat16)]
    pallas_call x0 -> x3, Pallas kernels: none -> 58.7 us  [the longest x1 32 us: local_block(): pl.pallas_call(make_front(n_experts, capacity, cap), out_shape=(sds((le,...]
    dot_general x9 -> x0, matrix products: 45.5 us -> none  [the longest x1 10.2 us: local_block(): jnp.einsum('erf,erd->efd', hidden, dy_rows, preferred_element_type=jnp.fl...]
    all_to_all x4 -> x0, starting transfers between devices: 16.1 us -> none  [the longest x2 8.95 us: dispatch(): recv_buf = lax.all_to_all(send_buf, 'ep', 0, 2, tiled=True)]
    reshape x8 -> x0, local copies, waits for them, and re-layouts: 7.95 us -> none  [the longest x2 4.16 us: combine(): send_buf = expert_rows.reshape(local_experts, ep_size, capacity, d_model)]
    unnamed x18 -> x17, local copies, waits for them, and re-layouts: 0.05 us -> 7 us
    all_to_all x4 -> x0, waiting for transfers between devices: 5.81 us -> none  [the longest x2 5.81 us: dispatch(): recv_buf = lax.all_to_all(send_buf, 'ep', 0, 2, tiled=True)]
    ppermute x0 -> x1, waiting for transfers between devices: none -> 2.4 us  [local_block(): srecv = lax.ppermute(speer, 'tp', [(0, 1), (1, 0)])]
  transfers between devices with their start and end apart: 4 -> 1, of which waited for: 1 -> 1; matrix products, arithmetic and copies ran while one was open for 17% -> 0% of each run, Pallas kernels for 0% -> 16%
where the time goes in v1:
time: 70.6 us; the launch traced here: 70.3 us
  Pallas kernels  58.7 us (83%)
  local copies, waits for them, and re-layouts  7 us (10%)
  waiting for transfers between devices  2.4 us (3%)
  starting transfers between devices  1.56 us (2%)
    pallas_call x1, Pallas kernels, local_block(): pl.pallas_call(make_front(n_experts, capacity, cap), out_shape=(sds((le,...  32 us
    pallas_call x1, Pallas kernels, local_block(): pl.pallas_call(make_back(n_experts, capacity, cap), out_shape=(sds((n, d_...  15.2 us
    pallas_call x1, Pallas kernels, local_block(): pl.pallas_call(grads_kernel, grid=(le, steps), out_shape=(sds((le, d_mode...  11.5 us
    unnamed x17, local copies, waits for them, and re-layouts  7 us
    ppermute x1, waiting for transfers between devices, local_block(): srecv = lax.ppermute(speer, 'tp', [(0, 1), (1, 0)])  2.4 us
    ppermute x1, starting transfers between devices, local_block(): srecv = lax.ppermute(speer, 'tp', [(0, 1), (1, 0)])  1.56 us
  transfers between devices with their start and end apart: 1, of which 1 were waited for; matrix products, arithmetic and copies ran while one was open for 0% of the time, Pallas kernels for 16%

profile of v1, /device:TPU:0, one launch (start us, length us, event | category | flops | bytes accessed | tf_op | source)
XLA Modules:
  0.0 70.3 jit_solution(2910704064964726230)
XLA Ops:
  0.6 0.0 copy-start
  0.6 1.0 %copy-done = bf16[256,1024]{1,0:T(8,128)(2,1)S(1)} copy-done((bf16[256,1024]{1,0:T(8,128)(2,1)S(1)}, bf16[256,1024]{1,0:T(8,128)(2,1)}, u32[]{:S(2)}) %copy-start) | copy-done | bytes 524312
  1.7 0.0 copy-start.1
  1.7 1.0 %copy-done.1 = bf16[256,1024]{1,0:T(8,128)(2,1)S(1)} copy-done((bf16[256,1024]{1,0:T(8,128)(2,1)S(1)}, bf16[256,1024]{1,0:T(8,128)(2,1)}, u32[]{:S(2)}) %copy-start.1) | copy-done | bytes 524312
  2.7 0.0 copy-start.2
  2.7 0.7 %copy-done.2 = bf16[1024,8]{0,1:T(8,128)(2,1)S(1)} copy-done((bf16[1024,8]{0,1:T(8,128)(2,1)S(1)}, bf16[1024,8]{0,1:T(8,128)(2,1)}, u32[]{:S(2)}) %copy-start.2) | copy-done | bytes 16408
  3.4 0.0 copy-start.4
  3.4 0.7 copy-done.4
  4.1 32.0 %front.1 = (bf16[2,160,2048]{2,1,0:T(8,128)(2,1)S(1)}, bf16[2,160,2048]{2,1,0:T(8,128)(2,1)}, bf16[2,160,1024]{2,1,0:T(8,128)(2,1)S(1)}, bf16[2,160,1024]{2,1,0:...) custom-call(bf16[256,1024]{1,0:T(8,128)(2,1)S(1)} %copy-done, ...), custom_call_target="tpu_custom_call" | custom-call | tf_op jit(solution)/shard_map/front/pallas_call | solution.py:282
  36.2 0.0 copy-start.3
  36.2 0.0 copy-start.5
  36.2 1.6 %collective-permute-start = (f32[2,160,512]{2,1,0:T(8,128)S(1)}, f32[2,160,512]{2,1,0:T(8,128)S(1)}, u32[]{:S(2)}, u32[]{:S(2)}) collective-permute-start(f32[2,160,512]{2,1,0:T(8,128)S(1)} %get-tuple-element.19), channel_id=1, source_target_pairs={{0,4},{4,0},{1,5},{5,1},{2,6},{6,2},{3,7},{7,3}} | collective-permute-start | bytes 1966088 | tf_op jit(solution)/shard_map/ppermute | solution.py:302
  37.7 0.0 copy-start.6
  37.7 1.3 %copy-done.6 = bf16[2,160,2048]{2,1,0:T(8,128)(2,1)S(1)} copy-done((bf16[2,160,2048]{2,1,0:T(8,128)(2,1)S(1)}, bf16[2,160,2048]{2,1,0:T(8,128)(2,1)}, u32[]{:S(2)}) %copy-start.6) | copy-done | bytes 1310744
  39.1 11.5 %weight_grads.1 = (f32[2,1024,2048]{2,1,0:T(8,128)}, f32[2,2048,1024]{2,1,0:T(8,128)}) custom-call(bf16[2,160,2048]{2,1,0:T(8,128)(2,1)S(1)} %get-tuple-element.22.h_ref, bf16[2,160,1024]{2,1,0:T(8,128)(2,1)S(1)} %get-tuple-element.23.dys_ref, bf16[2,160,1024]{2,1,0:T(8,128)(2,1)S(1)} %get-tuple-element.24.xs_ref, bf16[2,160,2048]{2,1,0:T(8,128)(2,1)S(1)} %copy-done.6), custom_call_target="tpu_custom_call" | custom-call | flops 2684354560 | bytes 33554432 | tf_op jit(solution)/shard_map/weight_grads/pallas_call | solution.py:306
  50.5 2.4 %collective-permute-done.srecv_ref = f32[2,160,512]{2,1,0:T(8,128)S(1)} collective-permute-done((f32[2,160,512]{2,1,0:T(8,128)S(1)}, f32[2,160,512]{2,1,0:T(8,128)S(1)}, u32[]{:S(2)}, u32[]{:S(2)}) %collective-permute-start) | collective-permute-done | bytes 655392 | tf_op jit(solution)/shard_map/ppermute | solution.py:302
  52.9 0.0 copy-done.3
  52.9 0.0 copy-done.5
  52.9 15.2 %back.1 = (bf16[256,1024]{1,0:T(8,128)(2,1)S(1)}, bf16[256,1024]{1,0:T(8,128)(2,1)S(1)}, f32[8,1024]{1,0:T(8,128)S(1)}) custom-call(bf16[256,1024]{1,0:T(8,128)(2,1)S(1)} %copy-done, bf16[256,1024]{1,0:T(8,128)(2,1)S(1)} %copy-done.1, bf16[8,1024]{1,0:T(8,128)(2,1)S(1)} %bitcast.6, s32[1,256]{1,0:T(1,128)S(1)} %bitcast.9, bf16[320,512]{1,0:T(8,128)(2,1)S(1)} %bitcast.4, ...), custom_call_target="tpu_custom_call" | custom-call | tf_op jit(solution)/shard_map/back/pallas_call | solution.py:319
  68.1 0.8 %copy.14 = bf16[256,1024]{1,0:T(8,128)(2,1)} copy(bf16[256,1024]{1,0:T(8,128)(2,1)S(1)} %get-tuple-element.34) | data formatting | bytes 1048576
  68.9 0.8 %copy.15 = bf16[256,1024]{1,0:T(8,128)(2,1)} copy(bf16[256,1024]{1,0:T(8,128)(2,1)S(1)} %get-tuple-element.35) | data formatting | bytes 1048576
  69.7 0.6 copy.16
Async XLA Ops:
  0.6 1.0 %copy-start = (bf16[256,1024]{1,0:T(8,128)(2,1)S(1)}, bf16[256,1024]{1,0:T(8,128)(2,1)}, u32[]{:S(2)}) copy-start(bf16[256,1024]{1,0:T(8,128)(2,1)} %x_ref.3) | copy-start | bytes 1572868
  1.7 1.0 %copy-start.1 = (bf16[256,1024]{1,0:T(8,128)(2,1)S(1)}, bf16[256,1024]{1,0:T(8,128)(2,1)}, u32[]{:S(2)}) copy-start(bf16[256,1024]{1,0:T(8,128)(2,1)} %gy_ref.3) | copy-start | bytes 1572868
  2.7 0.7 %copy-start.2 = (bf16[1024,8]{0,1:T(8,128)(2,1)S(1)}, bf16[1024,8]{0,1:T(8,128)(2,1)}, u32[]{:S(2)}) copy-start(bf16[1024,8]{0,1:T(8,128)(2,1)} %param.8) | copy-start | bytes 49156
  3.4 0.7 copy-start.4
  36.2 16.8 %copy-start.3 = (bf16[1024,8]{0,1:T(8,128)(2,1)S(1)}, bf16[1024,8]{0,1:T(8,128)(2,1)}, u32[]{:S(2)}) copy-start(bf16[1024,8]{0,1:T(8,128)(2,1)} %param.8) | copy-start | bytes 49156
  36.2 16.8 %copy-start.5 = (s32[256]{0:T(256)S(1)}, s32[256]{0:T(256)}, u32[]{:S(2)}) copy-start(s32[256]{0:T(256)} %param.11) | copy-start | bytes 3076
  36.2 16.7 %collective-permute-start = (f32[2,160,512]{2,1,0:T(8,128)S(1)}, f32[2,160,512]{2,1,0:T(8,128)S(1)}, u32[]{:S(2)}, u32[]{:S(2)}) collective-permute-start(f32[2,160,512]{2,1,0:T(8,128)S(1)} %get-tuple-element.19), channel_id=1, source_target_pairs={{0,4},{4,0},{1,5},{5,1},{2,6},{6,2},{3,7},{7,3}} | collective-permute-start | bytes 1966088 | tf_op jit(solution)/shard_map/ppermute | solution.py:302
  37.7 1.3 %copy-start.6 = (bf16[2,160,2048]{2,1,0:T(8,128)(2,1)S(1)}, bf16[2,160,2048]{2,1,0:T(8,128)(2,1)}, u32[]{:S(2)}) copy-start(bf16[2,160,2048]{2,1,0:T(8,128)(2,1)} %get-tuple-element.25.da_ref) | copy-start | bytes 3932164

commit v2 on v1

v2 whole, which is shorter than its diff:
```python
import jax
import jax.numpy as jnp
from jax import lax
from jax.experimental import pallas as pl
from jax.experimental.pallas import tpu as pltpu
from jax.sharding import PartitionSpec as P

MESH = pl.DeviceIdType.MESH
F32, BF16 = jnp.float32, jnp.bfloat16
CONTRACT_LAST = (((1,), (1,)), ((), ()))
CONTRACT_FIRST = (((0,), (0,)), ((), ()))
GELU_C = 0.7978845608028654
GELU_K = 0.044715


def mm(a, b, dims=(((1,), (0,)), ((), ()))):
    return lax.dot_general(a, b, dims, preferred_element_type=F32)


def ep_partners():
    ep = lax.axis_index("ep")
    cx, cc = ep // 2, ep % 2
    return [ep, 2 * cx + (1 - cc), 2 * (1 - cx) + cc, 2 * (1 - cx) + (1 - cc)]


def route(idx_row, capacity, n_experts, stride):
    n = idx_row.shape[1]
    expert = lax.broadcasted_iota(jnp.int32, (n_experts, n), 0)
    hot = jnp.where(expert == idx_row, 1.0, 0.0)
    earlier = lax.broadcasted_iota(jnp.int32, (n, n), 0)
    later = lax.broadcasted_iota(jnp.int32, (n, n), 1)
    upto = jnp.where(earlier <= later, 1.0, 0.0).astype(BF16)
    count = mm(hot.astype(BF16), upto)
    position = jnp.sum(hot * count, axis=0, keepdims=True) - 1.0
    slot = jnp.where(position < capacity, idx_row.astype(F32) * stride + position, -1.0)
    return hot, slot


def pick(slot, first, rows):
    n = slot.shape[1]
    row = (lax.broadcasted_iota(jnp.int32, (rows, n), 0) + first).astype(F32)
    return jnp.where(row == slot, 1.0, 0.0).astype(BF16)


def gate_of(x, wgt, hot):
    n_experts = hot.shape[0]
    logits = mm(x, wgt, CONTRACT_LAST)
    e = jnp.exp(logits - jnp.max(logits, axis=1, keepdims=True))
    prob = e / jnp.sum(e, axis=1, keepdims=True)
    eye = jnp.where(
        lax.broadcasted_iota(jnp.int32, (n_experts, n_experts), 0)
        == lax.broadcasted_iota(jnp.int32, (n_experts, n_experts), 1), 1.0, 0.0)
    chosen = mm(hot.astype(BF16), eye.astype(BF16), CONTRACT_FIRST)
    gate = jnp.sum(chosen * prob, axis=1, keepdims=True)
    return prob, chosen, gate


def enter(peers, tp_peer):
    barrier = pltpu.get_barrier_semaphore()
    for r in (1, 2, 3):
        pl.semaphore_signal(barrier, inc=1, device_id={"ep": peers[r]}, device_id_type=MESH)
    pl.semaphore_signal(barrier, inc=1, device_id={"tp": tp_peer}, device_id_type=MESH)
    return barrier


def send(src, dst, ssem, rsem, device):
    copy = pltpu.make_async_remote_copy(
        src_ref=src, dst_ref=dst, send_sem=ssem, recv_sem=rsem, device_id=device, device_id_type=MESH)
    copy.start()
    return copy


def pair(lo, hi, e, cap):
    a = lo.astype(F32)[e * cap:(e + 1) * cap]
    b = hi.astype(F32)[e * cap:(e + 1) * cap]
    return jnp.concatenate([a, b], axis=0).astype(BF16)


def make_front(n_experts, capacity, cap):
    blk = 2 * cap

    def front(x_hbm, gy_hbm, wgt_hbm, idx_hbm, wi_hbm, wo_hbm,
              h_ref, da_ref, xs_ref, dys_ref, speer_ref, sown_ref, yhalf_ref, sfirst_ref,
              x_ref, gy_ref, wgt_ref, idx_ref, wi, wo, xsend, dysend, xrecv, dyrecv, gp,
              ypeer, yown, yrecv, yback, yland, s0peer, s0own, s0recv, s0back, s0land,
              in_sem, wsem, x_s, x_r, d_s, d_r, y_s, y_r, b_s, b_r, s_s, s_r, t_s, t_r):
        tp = lax.axis_index("tp")
        tp_peer = 1 - tp
        peers = ep_partners()
        half = x_ref.shape[1] // 2
        mine = pl.ds(pl.multiple_of(tp * half, half), half)
        theirs = pl.ds(pl.multiple_of(tp_peer * half, half), half)
        d_ff = wi.shape[2]
        with jax.named_scope("enter"):
            barrier = enter(peers, tp_peer)
            small = [pltpu.make_async_copy(src, dst, in_sem.at[k]) for k, (src, dst) in enumerate(
                ((idx_hbm, idx_ref), (x_hbm, x_ref), (wgt_hbm, wgt_ref), (gy_hbm, gy_ref)))]
            for copy in small:
                copy.start()
            loads = {}
            for e in range(2):
                loads["i", e] = pltpu.make_async_copy(wi_hbm.at[e], wi.at[e], wsem.at[0, e])
                loads["o", e] = pltpu.make_async_copy(wo_hbm.at[e], wo.at[e], wsem.at[1, e])
            for e in range(2):
                loads["i", e].start()
                loads["o", e].start()

        with jax.named_scope("route"):
            small[0].wait()
            hot, slot = route(idx_ref[...], capacity, n_experts, cap)
            picks = [pick(slot, peers[r] * blk, blk) for r in range(4)]
            small[1].wait()
            x = x_ref[...]
            for r in (2, 3, 1, 0):
                xsend[r] = mm(picks[r], x).astype(BF16)
        with jax.named_scope("barrier"):
            pl.semaphore_wait(barrier, 4)
        xc, dc = {}, {}
        with jax.named_scope("dispatch"):
            for r in (2, 3, 1):
                xc[r] = send(xsend.at[r], xrecv.at[r - 1], x_s.at[r - 1], x_r.at[r - 1], {"ep": peers[r]})
            small[2].wait()
            small[3].wait()
            _, _, gate = gate_of(x, wgt_ref[...], hot)
            dy = (gate * gy_ref[...].astype(F32)).astype(BF16)
            for r in (2, 3, 1, 0):
                dysend[r] = mm(picks[r], dy).astype(BF16)
                if r:
                    dc[r] = send(dysend.at[r], dyrecv.at[r - 1], d_s.at[r - 1], d_r.at[r - 1], {"ep": peers[r]})

        yc = {}

        def forward(g):
            rows = slice(g * blk, (g + 1) * blk)
            for e in range(2):
                lo = xsend[0] if g == 0 else xrecv[1]
                hi = xrecv[0] if g == 0 else xrecv[2]
                xs_ref[e, rows, :] = pair(lo, hi, e, cap)
            for e in range(2):
                with jax.named_scope(f"act#g={g}#e={e}"):
                    if g == 0:
                        loads["i", e].wait()
                    xg = xs_ref[e, rows, :]
                    step = d_ff // 2
                    for c in range(2):
                        cols = slice(c * step, (c + 1) * step)
                        a = mm(xg, wi[e, :, cols])
                        t = jnp.tanh(GELU_C * (a + GELU_K * (a * a * a)))
                        cdf = 0.5 * (1.0 + t)
                        h_ref[e, rows, cols] = (a * cdf).astype(BF16)
                        gp[e, rows, cols] = cdf + (0.5 * a) * (1.0 - t * t) * (GELU_C + (3.0 * GELU_C * GELU_K) * (a * a))
                with jax.named_scope(f"ypeer#g={g}#e={e}"):
                    if g == 0:
                        loads["o", e].wait()
                    ypeer[g, e] = mm(h_ref[e, rows, :], wo[e, :, theirs])
                    yc[g, e] = send(ypeer.at[g, e], yrecv.at[g, e], y_s.at[g, e], y_r.at[g, e], {"tp": tp_peer})

        sc = []

        def backward(e):
            with jax.named_scope(f"dh#e={e}"):
                for g in range(2):
                    lo = dysend[0] if g == 0 else dyrecv[1]
                    hi = dyrecv[0] if g == 0 else dyrecv[2]
                    dys_ref[e, g * blk:(g + 1) * blk, :] = pair(lo, hi, e, cap)
                dyg = dys_ref[e]
                step = d_ff // 4
                for c in range(4):
                    cols = slice(c * step, (c + 1) * step)
                    dh = mm(dyg, wo[e, cols, :], CONTRACT_LAST)
                    da_ref[e, :, cols] = (dh * gp[e, :, cols]).astype(BF16)
            with jax.named_scope(f"s#e={e}"):
                dag = da_ref[e]
                if e == 0:
                    s0peer[...] = mm(dag, wi[e, theirs, :], CONTRACT_LAST)
                    sc.append(send(s0peer, s0recv, s_s, s_r, {"tp": tp_peer}))
                    s0own[...] = mm(dag, wi[e, mine, :], CONTRACT_LAST)
                else:
                    speer_ref[...] = mm(dag, wi[e, theirs, :], CONTRACT_LAST)
                    sown_ref[...] = mm(dag, wi[e, mine, :], CONTRACT_LAST)

        bc = {}

        def give_back(g):
            for e in range(2):
                yc[g, e].wait()
            rows = slice(g * blk, (g + 1) * blk)
            both = [yown[e, rows, :] + yrecv[g, e] for e in range(2)]
            for q in range(2):
                r = 2 * g + q
                block = jnp.concatenate([both[e][q * cap:(q + 1) * cap] for e in range(2)], axis=0).astype(BF16)
                if r == 0:
                    yland[0:blk, :] = block
                else:
                    yback[r - 1] = block
                    bc[r] = send(yback.at[r - 1], yland.at[r * blk:(r + 1) * blk, :], b_s.at[r - 1], b_r.at[r - 1],
                                 {"ep": peers[r]})

        with jax.named_scope("wait_near"):
            xc[1].wait()
        forward(0)
        with jax.named_scope("wait_far"):
            xc[2].wait()
            xc[3].wait()
        forward(1)
        with jax.named_scope("yown"):
            for e in range(2):
                yown[e] = mm(h_ref[e], wo[e, :, mine])
        with jax.named_scope("wait_dy"):
            for r in (1, 2, 3):
                dc[r].wait()
        backward(0)
        with jax.named_scope("give_back#g=0"):
            give_back(0)
        backward(1)
        with jax.named_scope("give_back#g=1"):
            give_back(1)
        with jax.named_scope("s0_back"):
            sc[0].wait()
            total = s0own[...] + s0recv[...]
            tc = {}
            sfirst_ref[0:cap, :] = total[0:cap].astype(BF16)
            for r in (2, 3, 1):
                s0back[r - 1] = total[r * cap:(r + 1) * cap].astype(BF16)
                tc[r] = send(s0back.at[r - 1], s0land.at[r - 1], t_s.at[r - 1], t_r.at[r - 1], {"ep": peers[r]})
        with jax.named_scope("y_tok"):
            for r in (1, 2, 3):
                bc[r].wait()
            yhalf_ref[...] = mm(jnp.concatenate(picks, axis=0), yland[...], CONTRACT_FIRST).astype(BF16)
        with jax.named_scope("s0_land"):
            for r in (1, 2, 3):
                tc[r].wait()
            sfirst_ref[...] = jnp.concatenate(
                [total[0:cap]] + [s0land[r - 1].astype(F32) for r in (1, 2, 3)], axis=0).astype(BF16)

    return front


def grads_kernel(h_ref, dys_ref, xs_ref, da_ref, dwi_ref, dwo_ref):
    dwo_ref[0] = mm(h_ref[0], dys_ref[0], CONTRACT_FIRST)
    dwi_ref[0] = mm(xs_ref[0], da_ref[0], CONTRACT_FIRST)


def make_back(n_experts, capacity, cap):
    blk = 2 * cap

    def back(x_ref, gy_ref, wgt_ref, idx_ref, ymine_ref, ytheirs_ref, sfirst_ref, sown_ref, srecv_ref,
             out_ref, dx_ref, dwgt_ref,
             sback, sland, dxsend, dxland, dwg,
             b_s, b_r, x_s, x_r, w_s, w_r):
        tp = lax.axis_index("tp")
        ep = lax.axis_index("ep")
        tp_peer = 1 - tp
        peers = ep_partners()
        half = x_ref.shape[1] // 2
        mine = pl.ds(pl.multiple_of(tp * half, half), half)
        theirs = pl.ds(pl.multiple_of(tp_peer * half, half), half)
        with jax.named_scope("enter"):
            barrier = enter(peers, tp_peer)
            total = sown_ref[...] + srecv_ref[...]
            for r in (2, 3, 1):
                sback[r - 1] = total[r * cap:(r + 1) * cap].astype(BF16)
            pl.semaphore_wait(barrier, 4)
        bc, wc = {}, {}
        with jax.named_scope("s_back"):
            for r in (2, 3, 1):
                bc[r] = send(sback.at[r - 1], sland.at[r - 1], b_s.at[r - 1], b_r.at[r - 1], {"ep": peers[r]})
        with jax.named_scope("router"):
            hot, slot = route(idx_ref[...], capacity, n_experts, cap)
            x = x_ref[...]
            prob, chosen, gate = gate_of(x, wgt_ref[...], hot)
            y_mine = ymine_ref[...].astype(F32)
            y_theirs = ytheirs_ref[...].astype(F32)
            dgate = (jnp.sum(gy_ref[:, mine].astype(F32) * y_mine, axis=1, keepdims=True)
                     + jnp.sum(gy_ref[:, theirs].astype(F32) * y_theirs, axis=1, keepdims=True))
            dlogits = (dgate * prob * (chosen - gate)).astype(BF16)
            dwg[ep] = mm(dlogits, x, CONTRACT_FIRST)
            for r in (2, 3, 1):
                wc[r] = send(dwg.at[ep], dwg.at[ep], w_s.at[r - 1], w_r.at[r - 1], {"ep": peers[r]})
            rgrad = mm(dlogits, wgt_ref[:, mine])
            even = jnp.concatenate([pick(slot, peers[r] * blk, cap) for r in range(4)], axis=0)
            odd = jnp.concatenate([pick(slot, peers[r] * blk + cap, cap) for r in range(4)], axis=0)
            s_even = mm(even, sfirst_ref[...], CONTRACT_FIRST)
        with jax.named_scope("s_wait"):
            for r in (1, 2, 3):
                bc[r].wait()
        with jax.named_scope("dx"):
            second = jnp.concatenate(
                [total[0:cap]] + [sland[r - 1].astype(F32) for r in (1, 2, 3)], axis=0).astype(BF16)
            dx_mine = (s_even + mm(odd, second, CONTRACT_FIRST) + rgrad).astype(BF16)
            dxsend[...] = dx_mine
            xc = send(dxsend, dxland, x_s, x_r, {"tp": tp_peer})
        with jax.named_scope("out"):
            dx_ref[:, mine] = dx_mine
            out_ref[:, mine] = (gate * y_mine).astype(BF16)
            out_ref[:, theirs] = (gate * y_theirs).astype(BF16)
            for r in (1, 2, 3):
                wc[r].wait()
            dwgt_ref[...] = (dwg[0] + dwg[1]) + (dwg[2] + dwg[3])
        with jax.named_scope("dx_wait"):
            xc.wait()
            dx_ref[:, theirs] = dxland[...]

    return back


def finish(out_ref, dx_ref, dwgt_ref, out_hbm, dx_hbm, dwgt_hbm, sem):
    copies = [pltpu.make_async_copy(src, dst, sem.at[k]) for k, (src, dst) in enumerate(
        ((out_ref, out_hbm), (dx_ref, dx_hbm), (dwgt_ref, dwgt_hbm)))]
    for copy in copies:
        copy.start()
    for copy in copies:
        copy.wait()


def solution(mesh):
    row_spec = P(("dp", "ep"), None)
    vmem = pl.BlockSpec(memory_space=pltpu.VMEM)
    hbm = pl.BlockSpec(memory_space=pltpu.HBM)

    def local_block(tokens, grad_out, w_router, w_in, w_out, expert_ids):
        n, d_model = tokens.shape
        n_experts = w_router.shape[1]
        le, _, d_ff = w_in.shape
        capacity = (6 * n + 5 * n_experts - 1) // (5 * n_experts)
        cap = -(-capacity // 8) * 8
        blk = le * cap
        rows = 4 * cap
        half = d_model // 2
        wgt = w_router.T
        idx_row = expert_ids.reshape(1, n)
        sds = jax.ShapeDtypeStruct
        dma = pltpu.SemaphoreType.DMA

        h, da, xs, dys, speer, sown, ymine, sfirst = pl.pallas_call(
            make_front(n_experts, capacity, cap),
            out_shape=(sds((le, rows, d_ff), BF16), sds((le, rows, d_ff), BF16), sds((le, rows, d_model), BF16),
                       sds((le, rows, d_model), BF16), sds((rows, half), F32), sds((rows, half), F32),
                       sds((n, half), BF16), sds((rows, half), BF16)),
            in_specs=[hbm] * 6,
            out_specs=(vmem,) * 8,
            scratch_shapes=[
                pltpu.VMEM((n, d_model), BF16), pltpu.VMEM((n, d_model), BF16), pltpu.VMEM((n_experts, d_model), BF16),
                pltpu.VMEM((1, n), jnp.int32),
                pltpu.VMEM((le, d_model, d_ff), BF16), pltpu.VMEM((le, d_ff, d_model), BF16),
                pltpu.VMEM((4, blk, d_model), BF16), pltpu.VMEM((4, blk, d_model), BF16),
                pltpu.VMEM((3, blk, d_model), BF16), pltpu.VMEM((3, blk, d_model), BF16),
                pltpu.VMEM((le, rows, d_ff), F32),
                pltpu.VMEM((2, le, blk, half), F32), pltpu.VMEM((le, rows, half), F32), pltpu.VMEM((2, le, blk, half), F32),
                pltpu.VMEM((3, blk, half), BF16), pltpu.VMEM((4 * blk, half), BF16),
                pltpu.VMEM((rows, half), F32), pltpu.VMEM((rows, half), F32), pltpu.VMEM((rows, half), F32),
                pltpu.VMEM((3, cap, half), BF16), pltpu.VMEM((3, cap, half), BF16),
                dma((4,)), dma((2, le)), dma((3,)), dma((3,)), dma((3,)), dma((3,)), dma((2, le)), dma((2, le)),
                dma((3,)), dma((3,)), dma, dma, dma((3,)), dma((3,)),
            ],
            compiler_params=pltpu.CompilerParams(collective_id=0, has_side_effects=True, vmem_limit_bytes=40 * 2**20),
            name="front",
        )(*[pltpu.with_memory_space_constraint(v, pltpu.HBM) for v in (tokens, grad_out, wgt, idx_row, w_in, w_out)])

        swap = [(0, 1), (1, 0)]
        srecv = lax.ppermute(speer, "tp", swap)
        ytheirs = lax.ppermute(ymine, "tp", swap)

        steps = 4
        hs, ms = d_ff // steps, d_model // steps
        dwi, dwo = pl.pallas_call(
            grads_kernel,
            grid=(le, steps),
            out_shape=(sds((le, d_model, d_ff), F32), sds((le, d_ff, d_model), F32)),
            in_specs=[pl.BlockSpec((1, rows, hs), lambda e, c: (e, 0, c)), pl.BlockSpec((1, rows, d_model), lambda e, c: (e, 0, 0)),
                      pl.BlockSpec((1, rows, ms), lambda e, c: (e, 0, c)), pl.BlockSpec((1, rows, d_ff), lambda e, c: (e, 0, 0))],
            out_specs=(pl.BlockSpec((1, ms, d_ff), lambda e, c: (e, c, 0)), pl.BlockSpec((1, hs, d_model), lambda e, c: (e, c, 0))),
            cost_estimate=pl.CostEstimate(flops=4 * le * rows * d_model * d_ff, bytes_accessed=8 * le * d_model * d_ff,
                                          transcendentals=0),
            compiler_params=pltpu.CompilerParams(vmem_limit_bytes=24 * 2**20),
            name="weight_grads",
        )(h, dys, xs, da)

        ends = (sds((n, d_model), BF16), sds((n, d_model), BF16), sds((n_experts, d_model), F32))
        parts = pl.pallas_call(
            make_back(n_experts, capacity, cap),
            out_shape=ends,
            in_specs=[vmem] * 9,
            out_specs=(vmem,) * 3,
            scratch_shapes=[
                pltpu.VMEM((3, cap, half), BF16), pltpu.VMEM((3, cap, half), BF16),
                pltpu.VMEM((n, half), BF16), pltpu.VMEM((n, half), BF16),
                pltpu.VMEM((4, n_experts, d_model), F32),
                dma((3,)), dma((3,)), dma, dma, dma((3,)), dma((3,)),
            ],
            compiler_params=pltpu.CompilerParams(collective_id=1, has_side_effects=True, vmem_limit_bytes=24 * 2**20),
            name="back",
        )(tokens, grad_out, wgt, idx_row, ymine, ytheirs, sfirst, sown, srecv)
        out, dx, dwgt = pl.pallas_call(
            finish, out_shape=ends, in_specs=[vmem] * 3, out_specs=(hbm,) * 3, scratch_shapes=[dma((3,))],
            compiler_params=pltpu.CompilerParams(vmem_limit_bytes=8 * 2**20), name="finish",
        )(*parts)
        return out, dx, dwi, dwo, dwgt.T

    in_specs = (row_spec, row_spec, P(None, None), P("ep", None, "tp"), P("ep", "tp", None), P(("dp", "ep")))
    out_specs = (row_spec, row_spec, P(("dp", "ep"), None, "tp"), P(("dp", "ep"), "tp", None), P("dp", None))
    return jax.shard_map(local_block, mesh=mesh, in_specs=in_specs, out_specs=out_specs, check_vma=False)
```

time: 70.6 us -> 66.8 us (0.946)
  local copies, waits for them, and re-layouts: 7 us -> 0.03 us
  Pallas kernels: 58.7 us -> 61.9 us
    unnamed x17 -> x8, local copies, waits for them, and re-layouts: 7 us -> 0.03 us
    pallas_call x1, Pallas kernels: 32 us -> 36.8 us  [local_block(): pl.pallas_call(make_front(n_experts, capacity, cap), out_shape=(sds((le,...]
    pallas_call x1 -> x2, Pallas kernels: 15.2 us -> 13.6 us  [the longest x1 12.7 us: local_block(): pl.pallas_call(make_back(n_experts, capacity, cap), out_shape=ends, in_sp...]
    ppermute x1 -> x2, starting transfers between devices: 1.56 us -> 2.05 us  [the longest x1 1.52 us: local_block(): ytheirs = lax.ppermute(ymine, 'tp', swap)]
    ppermute x1 -> x2, waiting for transfers between devices: 2.4 us -> 2.01 us  [the longest x1 2 us: local_block(): ytheirs = lax.ppermute(ymine, 'tp', swap)]
  transfers between devices with their start and end apart: 1 -> 2, of which waited for: 1 -> 1; matrix products, arithmetic and copies ran while one was open for 0% -> 0% of each run, Pallas kernels for 16% -> 17%
where the time goes in v2:
time: 66.8 us; the launch traced here: 66.6 us
  Pallas kernels  61.9 us (93%)
  starting transfers between devices  2.05 us (3%)
  waiting for transfers between devices  2.01 us (3%)
  between operations  0.7 us (1%)
    pallas_call x1, Pallas kernels, local_block(): pl.pallas_call(make_front(n_experts, capacity, cap), out_shape=(sds((le,...  36.8 us
    pallas_call x1, Pallas kernels, local_block(): pl.pallas_call(make_back(n_experts, capacity, cap), out_shape=ends, in_sp...  12.7 us
    pallas_call x1, Pallas kernels, local_block(): pl.pallas_call(grads_kernel, grid=(le, steps), out_shape=(sds((le, d_mode...  11.5 us
    ppermute x1, waiting for transfers between devices, local_block(): ytheirs = lax.ppermute(ymine, 'tp', swap)  2 us
    ppermute x1, starting transfers between devices, local_block(): ytheirs = lax.ppermute(ymine, 'tp', swap)  1.52 us
  transfers between devices with their start and end apart: 2, of which 1 were waited for; matrix products, arithmetic and copies ran while one was open for 0% of the time, Pallas kernels for 17%

profile of v2, /device:TPU:0, one launch (start us, length us, event | category | flops | bytes accessed | tf_op | source)
XLA Modules:
  0.0 66.6 jit_solution(12453341300985662340)
XLA Ops:
  0.6 36.8 %front.1 = (bf16[2,160,2048]{2,1,0:T(8,128)(2,1)S(1)}, bf16[2,160,2048]{2,1,0:T(8,128)(2,1)S(1)}, bf16[2,160,1024]{2,1,0:T(8,128)(2,1)S(1)}, bf16[2,160,1024]{2,...) custom-call(bf16[256,1024]{1,0:T(8,128)(2,1)} %x_ref.1, ...), custom_call_target="tpu_custom_call" | custom-call | tf_op jit(solution)/shard_map/front/pallas_call | solution.py:335
  37.4 0.0 copy-start
  37.4 0.0 copy-start.1
  37.4 0.0 copy-start.2
  37.4 0.0 copy-start.3
  37.4 0.5 collective-permute-start.1
  38.0 1.5 %collective-permute-start = (bf16[256,512]{1,0:T(8,128)(2,1)S(1)}, bf16[256,512]{1,0:T(8,128)(2,1)S(1)}, u32[]{:S(2)}, u32[]{:S(2)}) collective-permute-start(bf16[256,512]{1,0:T(8,128)(2,1)S(1)} %get-tuple-element.21.ymine_ref), channel_id=1, source_target_pairs={{0,4},{4,0},{1,5},{5,1},{2,6},{6,2},{3,7},{7,3}} | collective-permute-start | bytes 786440 | tf_op jit(solution)/shard_map/ppermute | solution.py:362
  39.5 11.5 %weight_grads.1 = (f32[2,1024,2048]{2,1,0:T(8,128)}, f32[2,2048,1024]{2,1,0:T(8,128)}) custom-call(bf16[2,160,2048]{2,1,0:T(8,128)(2,1)S(1)} %get-tuple-element.30.h_ref, bf16[2,160,1024]{2,1,0:T(8,128)(2,1)S(1)} %get-tuple-element.31.dys_ref, bf16[2,160,1024]{2,1,0:T(8,128)(2,1)S(1)} %get-tuple-element.32.xs_ref, ...), custom_call_target="tpu_custom_call" | custom-call | flops 2684354560 | bytes 33554432 | tf_op jit(solution)/shard_map/weight_grads/pallas_call | solution.py:366
  50.9 2.0 %collective-permute-done.ytheirs_ref = bf16[256,512]{1,0:T(8,128)(2,1)S(1)} collective-permute-done((bf16[256,512]{1,0:T(8,128)(2,1)S(1)}, bf16[256,512]{1,0:T(8,128)(2,1)S(1)}, u32[]{:S(2)}, u32[]{:S(2)}) %collective-permute-start) | collective-permute-done | bytes 262176 | tf_op jit(solution)/shard_map/ppermute | solution.py:362
  53.0 0.0 collective-permute-done.1.srecv_ref
  53.0 0.0 copy-done
  53.0 0.0 copy-done.1
  53.0 0.0 copy-done.2
  53.0 0.0 copy-done.3
  53.0 12.7 %back.1 = (bf16[256,1024]{1,0:T(8,128)(2,1)S(1)}, bf16[256,1024]{1,0:T(8,128)(2,1)S(1)}, f32[8,1024]{1,0:T(8,128)S(1)}) custom-call(bf16[256,1024]{1,0:T(8,128)(2,1)S(1)} %copy-done, bf16[256,1024]{1,0:T(8,128)(2,1)S(1)} %copy-done.1, bf16[8,1024]{1,0:T(8,128)(2,1)S(1)} %bitcast.4, s32[1,256]{1,0:T(1,128)S(1)} %bitcast.6, ...), custom_call_target="tpu_custom_call" | custom-call | tf_op jit(solution)/shard_map/back/pallas_call | solution.py:380
  65.6 1.0 %finish.1 = (bf16[256,1024]{1,0:T(8,128)(2,1)}, bf16[256,1024]{1,0:T(8,128)(2,1)}, f32[8,1024]{1,0:T(8,128)}) custom-call(bf16[256,1024]{1,0:T(8,128)(2,1)S(1)} %get-tuple-element.25.out_ref, bf16[256,1024]{1,0:T(8,128)(2,1)S(1)} %get-tuple-element.26.dx_ref, f32[8,1024]{1,0:T(8,128)S(1)} %get-tuple-element.27.dwgt_ref), custom_call_target="tpu_custom_call" | custom-call | tf_op jit(solution)/shard_map/finish/pallas_call | solution.py:394
Async XLA Ops:
  37.4 15.6 %copy-start = (bf16[256,1024]{1,0:T(8,128)(2,1)S(1)}, bf16[256,1024]{1,0:T(8,128)(2,1)}, u32[]{:S(2)}) copy-start(bf16[256,1024]{1,0:T(8,128)(2,1)} %x_ref.1) | copy-start | bytes 1572868
  37.4 15.6 %copy-start.1 = (bf16[256,1024]{1,0:T(8,128)(2,1)S(1)}, bf16[256,1024]{1,0:T(8,128)(2,1)}, u32[]{:S(2)}) copy-start(bf16[256,1024]{1,0:T(8,128)(2,1)} %gy_ref.1) | copy-start | bytes 1572868
  37.4 15.5 %copy-start.2 = (bf16[1024,8]{0,1:T(8,128)(2,1)S(1)}, bf16[1024,8]{0,1:T(8,128)(2,1)}, u32[]{:S(2)}) copy-start(bf16[1024,8]{0,1:T(8,128)(2,1)} %param.8) | copy-start | bytes 49156
  37.4 15.5 %copy-start.3 = (s32[256]{0:T(256)S(1)}, s32[256]{0:T(256)}, u32[]{:S(2)}) copy-start(s32[256]{0:T(256)} %param.11) | copy-start | bytes 3076
  37.4 15.5 %collective-permute-start.1 = (f32[160,512]{1,0:T(8,128)S(1)}, f32[160,512]{1,0:T(8,128)S(1)}, u32[]{:S(2)}, u32[]{:S(2)}) collective-permute-start(f32[160,512]{1,0:T(8,128)S(1)} %get-tuple-element.24), channel_id=1, source_target_pairs={{0,4},{4,0},{1,5},{5,1},{2,6},{6,2},{3,7},{7,3}} | collective-permute-start | bytes 983048 | tf_op jit(solution)/shard_map/ppermute | solution.py:361
  38.0 15.0 %collective-permute-start = (bf16[256,512]{1,0:T(8,128)(2,1)S(1)}, bf16[256,512]{1,0:T(8,128)(2,1)S(1)}, u32[]{:S(2)}, u32[]{:S(2)}) collective-permute-start(bf16[256,512]{1,0:T(8,128)(2,1)S(1)} %get-tuple-element.21.ymine_ref), channel_id=1, source_target_pairs={{0,4},{4,0},{1,5},{5,1},{2,6},{6,2},{3,7},{7,3}} | collective-permute-start | bytes 786440 | tf_op jit(solution)/shard_map/ppermute | solution.py:362

commit v3 on v2

v3 whole, which is shorter than its diff:
```python
import jax
import jax.numpy as jnp
from jax import lax
from jax.experimental import pallas as pl
from jax.experimental.pallas import tpu as pltpu
from jax.sharding import PartitionSpec as P

MESH = pl.DeviceIdType.MESH
F32, BF16 = jnp.float32, jnp.bfloat16
CONTRACT_LAST = (((1,), (1,)), ((), ()))
CONTRACT_FIRST = (((0,), (0,)), ((), ()))
GELU_C = 0.7978845608028654
GELU_K = 0.044715


def mm(a, b, dims=(((1,), (0,)), ((), ()))):
    return lax.dot_general(a, b, dims, preferred_element_type=F32)


def ep_partners():
    ep = lax.axis_index("ep")
    cx, cc = ep // 2, ep % 2
    return [ep, 2 * cx + (1 - cc), 2 * (1 - cx) + cc, 2 * (1 - cx) + (1 - cc)]


def route(idx_row, capacity, n_experts, stride):
    n = idx_row.shape[1]
    expert = lax.broadcasted_iota(jnp.int32, (n_experts, n), 0)
    hot = jnp.where(expert == idx_row, 1.0, 0.0)
    earlier = lax.broadcasted_iota(jnp.int32, (n, n), 0)
    later = lax.broadcasted_iota(jnp.int32, (n, n), 1)
    upto = jnp.where(earlier <= later, 1.0, 0.0).astype(BF16)
    count = mm(hot.astype(BF16), upto)
    position = jnp.sum(hot * count, axis=0, keepdims=True) - 1.0
    slot = jnp.where(position < capacity, idx_row.astype(F32) * stride + position, -1.0)
    return hot, slot


def pick(slot, first, rows):
    n = slot.shape[1]
    row = (lax.broadcasted_iota(jnp.int32, (rows, n), 0) + first).astype(F32)
    return jnp.where(row == slot, 1.0, 0.0).astype(BF16)


def gate_of(x, wgt, hot):
    n_experts = hot.shape[0]
    logits = mm(x, wgt, CONTRACT_LAST)
    e = jnp.exp(logits - jnp.max(logits, axis=1, keepdims=True))
    prob = e / jnp.sum(e, axis=1, keepdims=True)
    eye = jnp.where(
        lax.broadcasted_iota(jnp.int32, (n_experts, n_experts), 0)
        == lax.broadcasted_iota(jnp.int32, (n_experts, n_experts), 1), 1.0, 0.0)
    chosen = mm(hot.astype(BF16), eye.astype(BF16), CONTRACT_FIRST)
    gate = jnp.sum(chosen * prob, axis=1, keepdims=True)
    return prob, chosen, gate


def enter(peers, tp_peer):
    barrier = pltpu.get_barrier_semaphore()
    for r in (1, 2, 3):
        pl.semaphore_signal(barrier, inc=1, device_id={"ep": peers[r]}, device_id_type=MESH)
    pl.semaphore_signal(barrier, inc=1, device_id={"tp": tp_peer}, device_id_type=MESH)
    return barrier


def send(src, dst, ssem, rsem, device):
    copy = pltpu.make_async_remote_copy(
        src_ref=src, dst_ref=dst, send_sem=ssem, recv_sem=rsem, device_id=device, device_id_type=MESH)
    copy.start()
    return copy


def pair(lo, hi, e, cap):
    a = lo.astype(F32)[e * cap:(e + 1) * cap]
    b = hi.astype(F32)[e * cap:(e + 1) * cap]
    return jnp.concatenate([a, b], axis=0).astype(BF16)


def make_front(n_experts, capacity, cap):
    blk = 2 * cap

    def front(x_hbm, gy_hbm, wgt_hbm, idx_hbm, wi_hbm, wo_hbm,
              h_ref, da_ref, xs_ref, dys_ref, speer_ref, sown_ref, ynear_ref, yfar0_ref, yfar1_ref,
              x_ref, gy_ref, wgt_ref, idx_ref, wi, wo, xsend, dysend, xrecv, dyrecv, gp,
              ypeer, yown, yrecv, yback, yland,
              in_sem, wsem, x_s, x_r, d_s, d_r, y_s, y_r, b_s, b_r):
        tp = lax.axis_index("tp")
        tp_peer = 1 - tp
        peers = ep_partners()
        half = x_ref.shape[1] // 2
        mine = pl.ds(pl.multiple_of(tp * half, half), half)
        theirs = pl.ds(pl.multiple_of(tp_peer * half, half), half)
        d_ff = wi.shape[2]
        near, far = slice(0, blk), slice(blk, 2 * blk)
        with jax.named_scope("enter"):
            barrier = enter(peers, tp_peer)
            small = [pltpu.make_async_copy(src, dst, in_sem.at[k]) for k, (src, dst) in enumerate(
                ((idx_hbm, idx_ref), (x_hbm, x_ref), (wgt_hbm, wgt_ref), (gy_hbm, gy_ref)))]
            for copy in small:
                copy.start()
            loads = {}
            for e in range(2):
                loads["i", e] = pltpu.make_async_copy(wi_hbm.at[e], wi.at[e], wsem.at[0, e])
                loads["o", e] = pltpu.make_async_copy(wo_hbm.at[e], wo.at[e], wsem.at[1, e])
            for e in range(2):
                loads["i", e].start()
                loads["o", e].start()

        xc, dc, yc = {}, {}, {}

        def send_x(r):
            xc[r] = send(xsend.at[r], xrecv.at[r - 1], x_s.at[r - 1], x_r.at[r - 1], {"ep": peers[r]})

        with jax.named_scope("route"):
            small[0].wait()
            hot, slot = route(idx_ref[...], capacity, n_experts, cap)
            picks = [pick(slot, peers[r] * blk, blk) for r in range(4)]
            small[1].wait()
            x = x_ref[...]
            for r in (2, 3):
                xsend[r] = mm(picks[r], x).astype(BF16)
        with jax.named_scope("barrier"):
            pl.semaphore_wait(barrier, 4)
        with jax.named_scope("dispatch_x"):
            send_x(2)
            send_x(3)
            xsend[1] = mm(picks[1], x).astype(BF16)
            send_x(1)
            xsend[0] = mm(picks[0], x).astype(BF16)
        with jax.named_scope("gate"):
            small[2].wait()
            small[3].wait()
            _, _, gate = gate_of(x, wgt_ref[...], hot)
            dy = (gate * gy_ref[...].astype(F32)).astype(BF16)

        def dispatch_dy():
            for r in (2, 3, 1, 0):
                dysend[r] = mm(picks[r], dy).astype(BF16)
                if r:
                    dc[r] = send(dysend.at[r], dyrecv.at[r - 1], d_s.at[r - 1], d_r.at[r - 1], {"ep": peers[r]})

        def forward(g, e):
            rows = far if g else near
            if g == 0:
                loads["i", e].wait()
            xg = xs_ref[e, rows, :]
            step = d_ff // 2
            for c in range(2):
                cols = slice(c * step, (c + 1) * step)
                a = mm(xg, wi[e, :, cols])
                t = jnp.tanh(GELU_C * (a + GELU_K * (a * a * a)))
                cdf = 0.5 * (1.0 + t)
                h_ref[e, rows, cols] = (a * cdf).astype(BF16)
                gp[e, rows, cols] = cdf + (0.5 * a) * (1.0 - t * t) * (GELU_C + (3.0 * GELU_C * GELU_K) * (a * a))
            if g == 0:
                loads["o", e].wait()
            ypeer[g, e] = mm(h_ref[e, rows, :], wo[e, :, theirs])
            yc[g, e] = send(ypeer.at[g, e], yrecv.at[g, e], y_s.at[g, e], y_r.at[g, e], {"tp": tp_peer})

        def backward(g, e):
            rows = far if g else near
            dyg = dys_ref[e, rows, :]
            step = d_ff // 4
            for c in range(4):
                cols = slice(c * step, (c + 1) * step)
                dh = mm(dyg, wo[e, cols, :], CONTRACT_LAST)
                da_ref[e, rows, cols] = (dh * gp[e, rows, cols]).astype(BF16)
            dag = da_ref[e, rows, :]
            speer_ref[e, rows, :] = mm(dag, wi[e, theirs, :], CONTRACT_LAST)
            sown_ref[e, rows, :] = mm(dag, wi[e, mine, :], CONTRACT_LAST)

        def y_blocks(g):
            for e in range(2):
                yc[g, e].wait()
            both = [yown[e, far if g else near, :] + yrecv[g, e] for e in range(2)]
            return [jnp.concatenate([both[e][q * cap:(q + 1) * cap] for e in range(2)], axis=0).astype(BF16) for q in range(2)]

        with jax.named_scope("wait_near"):
            xc[1].wait()
            for e in range(2):
                xs_ref[e, near, :] = pair(xsend[0], xrecv[0], e, cap)
        with jax.named_scope("fwd#g=0#e=0"):
            forward(0, 0)
        with jax.named_scope("dispatch_dy"):
            dispatch_dy()
        with jax.named_scope("fwd#g=0#e=1"):
            forward(0, 1)
        with jax.named_scope("bwd#g=0#e=0"):
            dc[1].wait()
            for e in range(2):
                dys_ref[e, near, :] = pair(dysend[0], dyrecv[0], e, cap)
            backward(0, 0)
        with jax.named_scope("wait_far"):
            xc[2].wait()
            xc[3].wait()
            for e in range(2):
                xs_ref[e, far, :] = pair(xrecv[1], xrecv[2], e, cap)
        with jax.named_scope("fwd#g=1#e=0"):
            forward(1, 0)
        with jax.named_scope("fwd#g=1#e=1"):
            forward(1, 1)
        with jax.named_scope("bwd#g=0#e=1"):
            backward(0, 1)
        with jax.named_scope("yown"):
            for e in range(2):
                yown[e] = mm(h_ref[e], wo[e, :, mine])
        with jax.named_scope("y_near"):
            kept, away = y_blocks(0)
            ynear_ref[near, :] = kept
            yback[...] = away
            bc = send(yback, yland, b_s, b_r, {"ep": peers[1]})
        with jax.named_scope("wait_dy"):
            dc[2].wait()
            dc[3].wait()
            for e in range(2):
                dys_ref[e, far, :] = pair(dyrecv[1], dyrecv[2], e, cap)
        with jax.named_scope("bwd#g=1#e=0"):
            backward(1, 0)
        with jax.named_scope("bwd#g=1#e=1"):
            backward(1, 1)
        with jax.named_scope("y_far"):
            bc.wait()
            ynear_ref[far, :] = yland[...]
            yfar0_ref[...], yfar1_ref[...] = y_blocks(1)

    return front


def grads_kernel(h_ref, dys_ref, xs_ref, da_ref, dwi_ref, dwo_ref):
    dwo_ref[0] = mm(h_ref[0], dys_ref[0], CONTRACT_FIRST)
    dwi_ref[0] = mm(xs_ref[0], da_ref[0], CONTRACT_FIRST)


def make_back(n_experts, capacity, cap):
    blk = 2 * cap

    def back(x_ref, gy_ref, wgt_ref, idx_ref, ynear_ref, yfar0_ref, yfar1_ref, sown_ref, srecv_ref,
             out_ref, dx_ref, dwgt_ref,
             ysend, yland, sback, sland, stsend, stland, dwg,
             y_s, y_r, b_s, b_r, x_s, x_r, w_s, w_r):
        tp = lax.axis_index("tp")
        ep = lax.axis_index("ep")
        tp_peer = 1 - tp
        peers = ep_partners()
        half = x_ref.shape[1] // 2
        mine = pl.ds(pl.multiple_of(tp * half, half), half)
        theirs = pl.ds(pl.multiple_of(tp_peer * half, half), half)
        with jax.named_scope("enter"):
            barrier = enter(peers, tp_peer)
            hot, slot = route(idx_ref[...], capacity, n_experts, cap)
            picks = jnp.concatenate([pick(slot, peers[r] * blk, blk) for r in range(4)], axis=0)
            y_rows = jnp.concatenate([ynear_ref[...], yfar0_ref[...], yfar1_ref[...]], axis=0)
            ysend[...] = mm(picks, y_rows, CONTRACT_FIRST).astype(BF16)
            pl.semaphore_wait(barrier, 4)
            yc = send(ysend, yland, y_s, y_r, {"tp": tp_peer})
        with jax.named_scope("s_back"):
            bc = {}
            for g in (1, 0):
                rows = slice(g * blk, (g + 1) * blk)
                both = [sown_ref[e, rows, :] + srecv_ref[e, rows, :] for e in range(2)]
                for q in range(2):
                    r = 2 * g + q
                    block = jnp.concatenate([both[e][q * cap:(q + 1) * cap] for e in range(2)], axis=0).astype(BF16)
                    if r == 0:
                        sland[0:blk, :] = block
                    else:
                        sback[r - 1] = block
                        bc[r] = send(sback.at[r - 1], sland.at[r * blk:(r + 1) * blk, :], b_s.at[r - 1], b_r.at[r - 1],
                                     {"ep": peers[r]})
        with jax.named_scope("gate"):
            x = x_ref[...]
            prob, chosen, gate = gate_of(x, wgt_ref[...], hot)
            y_mine = ysend[...].astype(F32)
            out_ref[:, mine] = (gate * y_mine).astype(BF16)
            dgate = jnp.sum(gy_ref[:, mine].astype(F32) * y_mine, axis=1, keepdims=True)
        with jax.named_scope("s_wait"):
            for r in (1, 2, 3):
                bc[r].wait()
            stsend[...] = mm(picks, sland[...], CONTRACT_FIRST).astype(BF16)
            xc = send(stsend, stland, x_s, x_r, {"tp": tp_peer})
        with jax.named_scope("y_wait"):
            yc.wait()
        with jax.named_scope("router"):
            y_theirs = yland[...].astype(F32)
            out_ref[:, theirs] = (gate * y_theirs).astype(BF16)
            dgate = dgate + jnp.sum(gy_ref[:, theirs].astype(F32) * y_theirs, axis=1, keepdims=True)
            dlogits = (dgate * prob * (chosen - gate)).astype(BF16)
            dwg[ep] = mm(dlogits, x, CONTRACT_FIRST)
            wc = {}
            for r in (2, 3, 1):
                wc[r] = send(dwg.at[ep], dwg.at[ep], w_s.at[r - 1], w_r.at[r - 1], {"ep": peers[r]})
            dx_ref[:, mine] = (stsend[...].astype(F32) + mm(dlogits, wgt_ref[:, mine])).astype(BF16)
            rgrad = mm(dlogits, wgt_ref[:, theirs])
        with jax.named_scope("dwg"):
            for r in (1, 2, 3):
                wc[r].wait()
            dwgt_ref[...] = (dwg[0] + dwg[1]) + (dwg[2] + dwg[3])
        with jax.named_scope("dx_wait"):
            xc.wait()
        with jax.named_scope("dx"):
            dx_ref[:, theirs] = (stland[...].astype(F32) + rgrad).astype(BF16)

    return back


def finish(out_ref, dx_ref, dwgt_ref, out_hbm, dx_hbm, dwgt_hbm, sem):
    copies = [pltpu.make_async_copy(src, dst, sem.at[k]) for k, (src, dst) in enumerate(
        ((out_ref, out_hbm), (dx_ref, dx_hbm), (dwgt_ref, dwgt_hbm)))]
    for copy in copies:
        copy.start()
    for copy in copies:
        copy.wait()


def solution(mesh):
    row_spec = P(("dp", "ep"), None)
    vmem = pl.BlockSpec(memory_space=pltpu.VMEM)
    hbm = pl.BlockSpec(memory_space=pltpu.HBM)

    def local_block(tokens, grad_out, w_router, w_in, w_out, expert_ids):
        n, d_model = tokens.shape
        n_experts = w_router.shape[1]
        le, _, d_ff = w_in.shape
        capacity = (6 * n + 5 * n_experts - 1) // (5 * n_experts)
        cap = -(-capacity // 8) * 8
        blk = le * cap
        rows = 4 * cap
        half = d_model // 2
        wgt = w_router.T
        idx_row = expert_ids.reshape(1, n)
        sds = jax.ShapeDtypeStruct
        dma = pltpu.SemaphoreType.DMA

        h, da, xs, dys, speer, sown, ynear, yfar0, yfar1 = pl.pallas_call(
            make_front(n_experts, capacity, cap),
            out_shape=(sds((le, rows, d_ff), BF16), sds((le, rows, d_ff), BF16), sds((le, rows, d_model), BF16),
                       sds((le, rows, d_model), BF16), sds((le, rows, half), F32), sds((le, rows, half), F32),
                       sds((2 * blk, half), BF16), sds((blk, half), BF16), sds((blk, half), BF16)),
            in_specs=[hbm] * 6,
            out_specs=(vmem,) * 9,
            scratch_shapes=[
                pltpu.VMEM((n, d_model), BF16), pltpu.VMEM((n, d_model), BF16), pltpu.VMEM((n_experts, d_model), BF16),
                pltpu.VMEM((1, n), jnp.int32),
                pltpu.VMEM((le, d_model, d_ff), BF16), pltpu.VMEM((le, d_ff, d_model), BF16),
                pltpu.VMEM((4, blk, d_model), BF16), pltpu.VMEM((4, blk, d_model), BF16),
                pltpu.VMEM((3, blk, d_model), BF16), pltpu.VMEM((3, blk, d_model), BF16),
                pltpu.VMEM((le, rows, d_ff), F32),
                pltpu.VMEM((2, le, blk, half), F32), pltpu.VMEM((le, rows, half), F32), pltpu.VMEM((2, le, blk, half), F32),
                pltpu.VMEM((blk, half), BF16), pltpu.VMEM((blk, half), BF16),
                dma((4,)), dma((2, le)), dma((3,)), dma((3,)), dma((3,)), dma((3,)), dma((2, le)), dma((2, le)), dma, dma,
            ],
            compiler_params=pltpu.CompilerParams(collective_id=0, has_side_effects=True, vmem_limit_bytes=40 * 2**20),
            name="front",
        )(*[pltpu.with_memory_space_constraint(v, pltpu.HBM) for v in (tokens, grad_out, wgt, idx_row, w_in, w_out)])

        srecv = lax.ppermute(speer, "tp", [(0, 1), (1, 0)])
        yland0 = lax.ppermute(yfar0, "ep", [(0, 2), (2, 0), (1, 3), (3, 1)])
        yland1 = lax.ppermute(yfar1, "ep", [(0, 3), (3, 0), (1, 2), (2, 1)])

        steps = 4
        hs, ms = d_ff // steps, d_model // steps
        dwi, dwo = pl.pallas_call(
            grads_kernel,
            grid=(le, steps),
            out_shape=(sds((le, d_model, d_ff), F32), sds((le, d_ff, d_model), F32)),
            in_specs=[pl.BlockSpec((1, rows, hs), lambda e, c: (e, 0, c)), pl.BlockSpec((1, rows, d_model), lambda e, c: (e, 0, 0)),
                      pl.BlockSpec((1, rows, ms), lambda e, c: (e, 0, c)), pl.BlockSpec((1, rows, d_ff), lambda e, c: (e, 0, 0))],
            out_specs=(pl.BlockSpec((1, ms, d_ff), lambda e, c: (e, c, 0)), pl.BlockSpec((1, hs, d_model), lambda e, c: (e, c, 0))),
            cost_estimate=pl.CostEstimate(flops=4 * le * rows * d_model * d_ff, bytes_accessed=8 * le * d_model * d_ff,
                                          transcendentals=0),
            compiler_params=pltpu.CompilerParams(vmem_limit_bytes=24 * 2**20),
            name="weight_grads",
        )(h, dys, xs, da)

        ends = (sds((n, d_model), BF16), sds((n, d_model), BF16), sds((n_experts, d_model), F32))
        parts = pl.pallas_call(
            make_back(n_experts, capacity, cap),
            out_shape=ends,
            in_specs=[vmem] * 9,
            out_specs=(vmem,) * 3,
            scratch_shapes=[
                pltpu.VMEM((n, half), BF16), pltpu.VMEM((n, half), BF16),
                pltpu.VMEM((3, blk, half), BF16), pltpu.VMEM((4 * blk, half), BF16),
                pltpu.VMEM((n, half), BF16), pltpu.VMEM((n, half), BF16),
                pltpu.VMEM((4, n_experts, d_model), F32),
                dma, dma, dma((3,)), dma((3,)), dma, dma, dma((3,)), dma((3,)),
            ],
            compiler_params=pltpu.CompilerParams(collective_id=1, has_side_effects=True, vmem_limit_bytes=24 * 2**20),
            name="back",
        )(tokens, grad_out, wgt, idx_row, ynear, yland0, yland1, sown, srecv)
        out, dx, dwgt = pl.pallas_call(
            finish, out_shape=ends, in_specs=[vmem] * 3, out_specs=(hbm,) * 3, scratch_shapes=[dma((3,))],
            compiler_params=pltpu.CompilerParams(vmem_limit_bytes=8 * 2**20), name="finish",
        )(*parts)
        return out, dx, dwi, dwo, dwgt.T

    in_specs = (row_spec, row_spec, P(None, None), P("ep", None, "tp"), P("ep", "tp", None), P(("dp", "ep")))
    out_specs = (row_spec, row_spec, P(("dp", "ep"), None, "tp"), P(("dp", "ep"), "tp", None), P("dp", None))
    return jax.shard_map(local_block, mesh=mesh, in_specs=in_specs, out_specs=out_specs, check_vma=False)
```

time: 66.8 us -> 60.5 us (0.906)
  Pallas kernels: 61.9 us -> 53.4 us
  starting transfers between devices: 2.05 us -> 3.58 us
    pallas_call x1, Pallas kernels: 36.8 us -> 25.6 us  [local_block(): pl.pallas_call(make_front(n_experts, capacity, cap), out_shape=(sds((le,...]
    pallas_call x1, Pallas kernels: 12.7 us -> 15.3 us  [local_block(): pl.pallas_call(make_back(n_experts, capacity, cap), out_shape=ends, in_sp...]
    ppermute x2 -> x3, starting transfers between devices: 2.05 us -> 3.58 us  [the longest x1 1.54 us: local_block(): srecv = lax.ppermute(speer, 'tp', [(0, 1), (1, 0)])]
    ppermute x2 -> x3, waiting for transfers between devices: 2.01 us -> 2.58 us  [the longest x1 2.58 us: local_block(): srecv = lax.ppermute(speer, 'tp', [(0, 1), (1, 0)])]
  transfers between devices with their start and end apart: 2 -> 3, of which waited for: 1 -> 1; matrix products, arithmetic and copies ran while one was open for 0% -> 0% of each run, Pallas kernels for 17% -> 19%
where the time goes in v3:
time: 60.5 us; the launch traced here: 60.4 us
  Pallas kernels  53.4 us (88%)
  starting transfers between devices  3.58 us (6%)
  waiting for transfers between devices  2.58 us (4%)
  between operations  0.86 us (1%)
    pallas_call x1, Pallas kernels, local_block(): pl.pallas_call(make_front(n_experts, capacity, cap), out_shape=(sds((le,...  25.6 us
    pallas_call x1, Pallas kernels, local_block(): pl.pallas_call(make_back(n_experts, capacity, cap), out_shape=ends, in_sp...  15.3 us
    pallas_call x1, Pallas kernels, local_block(): pl.pallas_call(grads_kernel, grid=(le, steps), out_shape=(sds((le, d_mode...  11.5 us
    ppermute x1, waiting for transfers between devices, local_block(): srecv = lax.ppermute(speer, 'tp', [(0, 1), (1, 0)])  2.58 us
    ppermute x1, starting transfers between devices, local_block(): srecv = lax.ppermute(speer, 'tp', [(0, 1), (1, 0)])  1.54 us
    ppermute x1, starting transfers between devices, local_block(): yland0 = lax.ppermute(yfar0, 'ep', [(0, 2), (2, 0), (1, 3), (3, 1)])  1.29 us
  transfers between devices with their start and end apart: 3, of which 1 were waited for; matrix products, arithmetic and copies ran while one was open for 0% of the time, Pallas kernels for 19%

profile of v3, /device:TPU:0, one launch (start us, length us, event | category | flops | bytes accessed | tf_op | source)
XLA Modules:
  0.0 60.4 jit_solution(14205982582939148939)
XLA Ops:
  0.6 25.6 %front.1 = (bf16[2,160,2048]{2,1,0:T(8,128)(2,1)S(1)}, bf16[2,160,2048]{2,1,0:T(8,128)(2,1)S(1)}, bf16[2,160,1024]{2,1,0:T(8,128)(2,1)S(1)}, bf16[2,160,1024]{2,...) custom-call(bf16[256,1024]{1,0:T(8,128)(2,1)} %x_ref.1, ...), custom_call_target="tpu_custom_call" | custom-call | tf_op jit(solution)/shard_map/front/pallas_call | solution.py:334
  26.3 0.0 copy-start
  26.3 0.0 copy-start.1
  26.3 0.0 copy-start.2
  26.3 0.0 copy-start.3
  26.3 1.5 %collective-permute-start.2 = (f32[2,160,512]{2,1,0:T(8,128)S(1)}, f32[2,160,512]{2,1,0:T(8,128)S(1)}, u32[]{:S(2)}, u32[]{:S(2)}) collective-permute-start(f32[2,160,512]{2,1,0:T(8,128)S(1)} %get-tuple-element.26), channel_id=1, source_target_pairs={{0,4},{4,0},{1,5},{5,1},{2,6},{6,2},{3,7},{7,3}} | collective-permute-start | bytes 1966088 | tf_op jit(solution)/shard_map/ppermute | solution.py:356
  27.9 1.3 %collective-permute-start = (bf16[80,512]{1,0:T(8,128)(2,1)S(1)}, bf16[80,512]{1,0:T(8,128)(2,1)S(1)}, u32[]{:S(2)}, u32[]{:S(2)}) collective-permute-start(bf16[80,512]{1,0:T(8,128)(2,1)S(1)} %get-tuple-element.23), channel_id=1, source_target_pairs={{0,2},{2,0},{1,3},{3,1},{4,6},{6,4},{5,7},{7,5}} | collective-permute-start | bytes 245768 | tf_op jit(solution)/shard_map/ppermute | solution.py:357
  29.1 0.8 %collective-permute-start.1 = (bf16[80,512]{1,0:T(8,128)(2,1)S(1)}, bf16[80,512]{1,0:T(8,128)(2,1)S(1)}, u32[]{:S(2)}, u32[]{:S(2)}) collective-permute-start(bf16[80,512]{1,0:T(8,128)(2,1)S(1)} %get-tuple-element.24), channel_id=1, source_target_pairs={{0,3},{3,0},{1,2},{2,1},{4,7},{7,4},{5,6},{6,5}} | collective-permute-start | bytes 245768 | tf_op jit(solution)/shard_map/ppermute | solution.py:358
  29.9 11.5 %weight_grads.1 = (f32[2,1024,2048]{2,1,0:T(8,128)}, f32[2,2048,1024]{2,1,0:T(8,128)}) custom-call(bf16[2,160,2048]{2,1,0:T(8,128)(2,1)S(1)} %get-tuple-element.32.h_ref, bf16[2,160,1024]{2,1,0:T(8,128)(2,1)S(1)} %get-tuple-element.33.dys_ref, bf16[2,160,1024]{2,1,0:T(8,128)(2,1)S(1)} %get-tuple-element.34.xs_ref, ...), custom_call_target="tpu_custom_call" | custom-call | flops 2684354560 | bytes 33554432 | tf_op jit(solution)/shard_map/weight_grads/pallas_call | solution.py:362
  41.4 0.0 collective-permute-done.yfar0_ref
  41.4 0.0 collective-permute-done.1.yfar1_ref
  41.4 2.6 %collective-permute-done.2.srecv_ref = f32[2,160,512]{2,1,0:T(8,128)S(1)} collective-permute-done((f32[2,160,512]{2,1,0:T(8,128)S(1)}, f32[2,160,512]{2,1,0:T(8,128)S(1)}, u32[]{:S(2)}, u32[]{:S(2)}) %collective-permute-start.2) | collective-permute-done | bytes 655392 | tf_op jit(solution)/shard_map/ppermute | solution.py:356
  44.0 0.0 copy-done
  44.0 0.0 copy-done.1
  44.0 0.0 copy-done.2
  44.0 0.0 copy-done.3
  44.0 15.3 %back.1 = (bf16[256,1024]{1,0:T(8,128)(2,1)S(1)}, bf16[256,1024]{1,0:T(8,128)(2,1)S(1)}, f32[8,1024]{1,0:T(8,128)S(1)}) custom-call(bf16[256,1024]{1,0:T(8,128)(2,1)S(1)} %copy-done, bf16[256,1024]{1,0:T(8,128)(2,1)S(1)} %copy-done.1, bf16[8,1024]{1,0:T(8,128)(2,1)S(1)} %bitcast.4, s32[1,256]{1,0:T(1,128)S(1)} %bitcast.6, ...), custom_call_target="tpu_custom_call" | custom-call | tf_op jit(solution)/shard_map/back/pallas_call | solution.py:376
  59.2 1.0 %finish.1 = (bf16[256,1024]{1,0:T(8,128)(2,1)}, bf16[256,1024]{1,0:T(8,128)(2,1)}, f32[8,1024]{1,0:T(8,128)}) custom-call(bf16[256,1024]{1,0:T(8,128)(2,1)S(1)} %get-tuple-element.27.out_ref, bf16[256,1024]{1,0:T(8,128)(2,1)S(1)} %get-tuple-element.28.dx_ref, f32[8,1024]{1,0:T(8,128)S(1)} %get-tuple-element.29.dwgt_ref), custom_call_target="tpu_custom_call" | custom-call | tf_op jit(solution)/shard_map/finish/pallas_call | solution.py:391
Async XLA Ops:
  26.3 17.7 %copy-start = (bf16[256,1024]{1,0:T(8,128)(2,1)S(1)}, bf16[256,1024]{1,0:T(8,128)(2,1)}, u32[]{:S(2)}) copy-start(bf16[256,1024]{1,0:T(8,128)(2,1)} %x_ref.1) | copy-start | bytes 1572868
  26.3 17.7 %copy-start.1 = (bf16[256,1024]{1,0:T(8,128)(2,1)S(1)}, bf16[256,1024]{1,0:T(8,128)(2,1)}, u32[]{:S(2)}) copy-start(bf16[256,1024]{1,0:T(8,128)(2,1)} %gy_ref.1) | copy-start | bytes 1572868
  26.3 17.7 %copy-start.2 = (bf16[1024,8]{0,1:T(8,128)(2,1)S(1)}, bf16[1024,8]{0,1:T(8,128)(2,1)}, u32[]{:S(2)}) copy-start(bf16[1024,8]{0,1:T(8,128)(2,1)} %param.8) | copy-start | bytes 49156
  26.3 17.7 %copy-start.3 = (s32[256]{0:T(256)S(1)}, s32[256]{0:T(256)}, u32[]{:S(2)}) copy-start(s32[256]{0:T(256)} %param.11) | copy-start | bytes 3076
  26.3 17.6 %collective-permute-start.2 = (f32[2,160,512]{2,1,0:T(8,128)S(1)}, f32[2,160,512]{2,1,0:T(8,128)S(1)}, u32[]{:S(2)}, u32[]{:S(2)}) collective-permute-start(f32[2,160,512]{2,1,0:T(8,128)S(1)} %get-tuple-element.26), channel_id=1, source_target_pairs={{0,4},{4,0},{1,5},{5,1},{2,6},{6,2},{3,7},{7,3}} | collective-permute-start | bytes 1966088 | tf_op jit(solution)/shard_map/ppermute | solution.py:356
  27.9 13.5 %collective-permute-start = (bf16[80,512]{1,0:T(8,128)(2,1)S(1)}, bf16[80,512]{1,0:T(8,128)(2,1)S(1)}, u32[]{:S(2)}, u32[]{:S(2)}) collective-permute-start(bf16[80,512]{1,0:T(8,128)(2,1)S(1)} %get-tuple-element.23), channel_id=1, source_target_pairs={{0,2},{2,0},{1,3},{3,1},{4,6},{6,4},{5,7},{7,5}} | collective-permute-start | bytes 245768 | tf_op jit(solution)/shard_map/ppermute | solution.py:357
  29.1 12.2 %collective-permute-start.1 = (bf16[80,512]{1,0:T(8,128)(2,1)S(1)}, bf16[80,512]{1,0:T(8,128)(2,1)S(1)}, u32[]{:S(2)}, u32[]{:S(2)}) collective-permute-start(bf16[80,512]{1,0:T(8,128)(2,1)S(1)} %get-tuple-element.24), channel_id=1, source_target_pairs={{0,3},{3,0},{1,2},{2,1},{4,7},{7,4},{5,6},{6,5}} | collective-permute-start | bytes 245768 | tf_op jit(solution)/shard_map/ppermute | solution.py:358

commit v4 on v3

--- a/solution.py
+++ b/solution.py
@@ -36,10 +36,11 @@
     return hot, slot
 
 
-def pick(slot, first, rows):
+def pick(slot, firsts, rows):
     n = slot.shape[1]
-    row = (lax.broadcasted_iota(jnp.int32, (rows, n), 0) + first).astype(F32)
-    return jnp.where(row == slot, 1.0, 0.0).astype(BF16)
+    row = lax.broadcasted_iota(jnp.int32, (rows, n), 0)
+    parts = [jnp.where((row + first).astype(F32) == slot, 1.0, 0.0) for first in firsts]
+    return jnp.concatenate(parts, axis=0).astype(BF16)
 
 
 def gate_of(x, wgt, hot):
@@ -70,18 +71,13 @@
     return copy
 
 
-def pair(lo, hi, e, cap):
-    a = lo.astype(F32)[e * cap:(e + 1) * cap]
-    b = hi.astype(F32)[e * cap:(e + 1) * cap]
-    return jnp.concatenate([a, b], axis=0).astype(BF16)
-
-
 def make_front(n_experts, capacity, cap):
     blk = 2 * cap
 
     def front(x_hbm, gy_hbm, wgt_hbm, idx_hbm, wi_hbm, wo_hbm,
               h_ref, da_ref, xs_ref, dys_ref, speer_ref, sown_ref, ynear_ref, yfar0_ref, yfar1_ref,
-              x_ref, gy_ref, wgt_ref, idx_ref, wi, wo, xsend, dysend, xrecv, dyrecv, gp,
+              picks_ref, prob_ref, chosen_ref,
+              x_ref, gy_ref, wgt_ref, idx_ref, wi, wo, xsend, dysend, gp,
               ypeer, yown, yrecv, yback, yland,
               in_sem, wsem, x_s, x_r, d_s, d_r, y_s, y_r, b_s, b_r):
         tp = lax.axis_index("tp")
@@ -91,13 +87,13 @@
         mine = pl.ds(pl.multiple_of(tp * half, half), half)
         theirs = pl.ds(pl.multiple_of(tp_peer * half, half), half)
         d_ff = wi.shape[2]
-        near, far = slice(0, blk), slice(blk, 2 * blk)
+        near, far, whole = slice(0, blk), slice(blk, 2 * blk), slice(0, 2 * blk)
         with jax.named_scope("enter"):
-            barrier = enter(peers, tp_peer)
             small = [pltpu.make_async_copy(src, dst, in_sem.at[k]) for k, (src, dst) in enumerate(
                 ((idx_hbm, idx_ref), (x_hbm, x_ref), (wgt_hbm, wgt_ref), (gy_hbm, gy_ref)))]
             for copy in small:
                 copy.start()
+            barrier = enter(peers, tp_peer)
             loads = {}
             for e in range(2):
                 loads["i", e] = pltpu.make_async_copy(wi_hbm.at[e], wi.at[e], wsem.at[0, e])
@@ -108,36 +104,39 @@
 
         xc, dc, yc = {}, {}, {}
 
-        def send_x(r):
-            xc[r] = send(xsend.at[r], xrecv.at[r - 1], x_s.at[r - 1], x_r.at[r - 1], {"ep": peers[r]})
+        def dispatch(v, g, e, buf, rows_ref, ssem, rsem, made):
+            first = [peers[2 * g + q] * blk + e * cap for q in range(2)]
+            rows = mm(pick(slot, first, cap), v)
+            for q in range(2):
+                r = 2 * g + q
+                part = rows[q * cap:(q + 1) * cap].astype(BF16)
+                if r == 0:
+                    rows_ref[e, 0:cap, :] = part
+                else:
+                    buf[r - 1, e] = part
+            return lambda: [made.__setitem__((r, e), send(
+                buf.at[r - 1, e], rows_ref.at[e, r * cap:(r + 1) * cap, :], ssem.at[r - 1, e], rsem.at[r - 1, e],
+                {"ep": peers[r]})) for r in (2 * g, 2 * g + 1) if r]
+
+        def dispatch_x(g, e):
+            return dispatch(x_ref[...], g, e, xsend, xs_ref, x_s, x_r, xc)
 
         with jax.named_scope("route"):
             small[0].wait()
             hot, slot = route(idx_ref[...], capacity, n_experts, cap)
-            picks = [pick(slot, peers[r] * blk, blk) for r in range(4)]
             small[1].wait()
-            x = x_ref[...]
-            for r in (2, 3):
-                xsend[r] = mm(picks[r], x).astype(BF16)
+            go = dispatch_x(1, 0)
         with jax.named_scope("barrier"):
             pl.semaphore_wait(barrier, 4)
         with jax.named_scope("dispatch_x"):
-            send_x(2)
-            send_x(3)
-            xsend[1] = mm(picks[1], x).astype(BF16)
-            send_x(1)
-            xsend[0] = mm(picks[0], x).astype(BF16)
+            go()
+            for e in range(2):
+                dispatch_x(0, e)()
+            dispatch_x(1, 1)()
         with jax.named_scope("gate"):
             small[2].wait()
-            small[3].wait()
-            _, _, gate = gate_of(x, wgt_ref[...], hot)
-            dy = (gate * gy_ref[...].astype(F32)).astype(BF16)
-
-        def dispatch_dy():
-            for r in (2, 3, 1, 0):
-                dysend[r] = mm(picks[r], dy).astype(BF16)
-                if r:
-                    dc[r] = send(dysend.at[r], dyrecv.at[r - 1], d_s.at[r - 1], d_r.at[r - 1], {"ep": peers[r]})
+            prob, chosen, gate = gate_of(x_ref[...], wgt_ref[...], hot)
+            prob_ref[...], chosen_ref[...] = prob, chosen
 
         def forward(g, e):
             rows = far if g else near
@@ -157,8 +156,7 @@
             ypeer[g, e] = mm(h_ref[e, rows, :], wo[e, :, theirs])
             yc[g, e] = send(ypeer.at[g, e], yrecv.at[g, e], y_s.at[g, e], y_r.at[g, e], {"tp": tp_peer})
 
-        def backward(g, e):
-            rows = far if g else near
+        def backward(rows, e):
             dyg = dys_ref[e, rows, :]
             step = d_ff // 4
             for c in range(4):
@@ -176,31 +174,33 @@
             return [jnp.concatenate([both[e][q * cap:(q + 1) * cap] for e in range(2)], axis=0).astype(BF16) for q in range(2)]
 
         with jax.named_scope("wait_near"):
-            xc[1].wait()
-            for e in range(2):
-                xs_ref[e, near, :] = pair(xsend[0], xrecv[0], e, cap)
+            xc[1, 0].wait()
         with jax.named_scope("fwd#g=0#e=0"):
             forward(0, 0)
         with jax.named_scope("dispatch_dy"):
-            dispatch_dy()
+            small[3].wait()
+            dy = (gate * gy_ref[...].astype(F32)).astype(BF16)
+            for g in (1, 0):
+                for e in range(2):
+                    dispatch(dy, g, e, dysend, dys_ref, d_s, d_r, dc)()
         with jax.named_scope("fwd#g=0#e=1"):
+            xc[1, 1].wait()
             forward(0, 1)
-        with jax.named_scope("bwd#g=0#e=0"):
-            dc[1].wait()
-            for e in range(2):
-                dys_ref[e, near, :] = pair(dysend[0], dyrecv[0], e, cap)
-            backward(0, 0)
-        with jax.named_scope("wait_far"):
-            xc[2].wait()
-            xc[3].wait()
-            for e in range(2):
-                xs_ref[e, far, :] = pair(xrecv[1], xrecv[2], e, cap)
+        with jax.named_scope("picks"):
+            picks_ref[...] = pick(slot, [peers[r] * blk for r in range(4)], blk)
+        with jax.named_scope("wait_far#e=0"):
+            xc[2, 0].wait()
+            xc[3, 0].wait()
         with jax.named_scope("fwd#g=1#e=0"):
             forward(1, 0)
+        with jax.named_scope("bwd#near#e=0"):
+            dc[1, 0].wait()
+            backward(near, 0)
+        with jax.named_scope("wait_far#e=1"):
+            xc[2, 1].wait()
+            xc[3, 1].wait()
         with jax.named_scope("fwd#g=1#e=1"):
             forward(1, 1)
-        with jax.named_scope("bwd#g=0#e=1"):
-            backward(0, 1)
         with jax.named_scope("yown"):
             for e in range(2):
                 yown[e] = mm(h_ref[e], wo[e, :, mine])
@@ -209,15 +209,16 @@
             ynear_ref[near, :] = kept
             yback[...] = away
             bc = send(yback, yland, b_s, b_r, {"ep": peers[1]})
-        with jax.named_scope("wait_dy"):
-            dc[2].wait()
-            dc[3].wait()
-            for e in range(2):
-                dys_ref[e, far, :] = pair(dyrecv[1], dyrecv[2], e, cap)
-        with jax.named_scope("bwd#g=1#e=0"):
-            backward(1, 0)
-        with jax.named_scope("bwd#g=1#e=1"):
-            backward(1, 1)
+        with jax.named_scope("wait_dy#e=0"):
+            dc[2, 0].wait()
+            dc[3, 0].wait()
+        with jax.named_scope("bwd#far#e=0"):
+            backward(far, 0)
+        with jax.named_scope("wait_dy#e=1"):
+            for r in (1, 2, 3):
+                dc[r, 1].wait()
+        with jax.named_scope("bwd#e=1"):
+            backward(whole, 1)
         with jax.named_scope("y_far"):
             bc.wait()
             ynear_ref[far, :] = yland[...]
@@ -231,10 +232,10 @@
     dwi_ref[0] = mm(xs_ref[0], da_ref[0], CONTRACT_FIRST)
 
 
-def make_back(n_experts, capacity, cap):
+def make_back(cap):
     blk = 2 * cap
 
-    def back(x_ref, gy_ref, wgt_ref, idx_ref, ynear_ref, yfar0_ref, yfar1_ref, sown_ref, srecv_ref,
+    def back(x_ref, gy_ref, wgt_ref, picks_ref, prob_ref, chosen_ref, ynear_ref, yfar0_ref, yfar1_ref, sown_ref, srecv_ref,
              out_ref, dx_ref, dwgt_ref,
              ysend, yland, sback, sland, stsend, stland, dwg,
              y_s, y_r, b_s, b_r, x_s, x_r, w_s, w_r):
@@ -247,8 +248,7 @@
         theirs = pl.ds(pl.multiple_of(tp_peer * half, half), half)
         with jax.named_scope("enter"):
             barrier = enter(peers, tp_peer)
-            hot, slot = route(idx_ref[...], capacity, n_experts, cap)
-            picks = jnp.concatenate([pick(slot, peers[r] * blk, blk) for r in range(4)], axis=0)
+            picks = picks_ref[...]
             y_rows = jnp.concatenate([ynear_ref[...], yfar0_ref[...], yfar1_ref[...]], axis=0)
             ysend[...] = mm(picks, y_rows, CONTRACT_FIRST).astype(BF16)
             pl.semaphore_wait(barrier, 4)
@@ -269,7 +269,8 @@
                                      {"ep": peers[r]})
         with jax.named_scope("gate"):
             x = x_ref[...]
-            prob, chosen, gate = gate_of(x, wgt_ref[...], hot)
+            prob, chosen = prob_ref[...], chosen_ref[...]
+            gate = jnp.sum(chosen * prob, axis=1, keepdims=True)
             y_mine = ysend[...].astype(F32)
             out_ref[:, mine] = (gate * y_mine).astype(BF16)
             dgate = jnp.sum(gy_ref[:, mine].astype(F32) * y_mine, axis=1, keepdims=True)
@@ -331,23 +332,23 @@
         sds = jax.ShapeDtypeStruct
         dma = pltpu.SemaphoreType.DMA
 
-        h, da, xs, dys, speer, sown, ynear, yfar0, yfar1 = pl.pallas_call(
+        h, da, xs, dys, speer, sown, ynear, yfar0, yfar1, picks, prob, chosen = pl.pallas_call(
             make_front(n_experts, capacity, cap),
             out_shape=(sds((le, rows, d_ff), BF16), sds((le, rows, d_ff), BF16), sds((le, rows, d_model), BF16),
                        sds((le, rows, d_model), BF16), sds((le, rows, half), F32), sds((le, rows, half), F32),
-                       sds((2 * blk, half), BF16), sds((blk, half), BF16), sds((blk, half), BF16)),
+                       sds((2 * blk, half), BF16), sds((blk, half), BF16), sds((blk, half), BF16),
+                       sds((4 * blk, n), BF16), sds((n, n_experts), F32), sds((n, n_experts), F32)),
             in_specs=[hbm] * 6,
-            out_specs=(vmem,) * 9,
+            out_specs=(vmem,) * 12,
             scratch_shapes=[
                 pltpu.VMEM((n, d_model), BF16), pltpu.VMEM((n, d_model), BF16), pltpu.VMEM((n_experts, d_model), BF16),
                 pltpu.VMEM((1, n), jnp.int32),
                 pltpu.VMEM((le, d_model, d_ff), BF16), pltpu.VMEM((le, d_ff, d_model), BF16),
-                pltpu.VMEM((4, blk, d_model), BF16), pltpu.VMEM((4, blk, d_model), BF16),
-                pltpu.VMEM((3, blk, d_model), BF16), pltpu.VMEM((3, blk, d_model), BF16),
+                pltpu.VMEM((3, le, cap, d_model), BF16), pltpu.VMEM((3, le, cap, d_model), BF16),
                 pltpu.VMEM((le, rows, d_ff), F32),
                 pltpu.VMEM((2, le, blk, half), F32), pltpu.VMEM((le, rows, half), F32), pltpu.VMEM((2, le, blk, half), F32),
                 pltpu.VMEM((blk, half), BF16), pltpu.VMEM((blk, half), BF16),
-                dma((4,)), dma((2, le)), dma((3,)), dma((3,)), dma((3,)), dma((3,)), dma((2, le)), dma((2, le)), dma, dma,
+                dma((4,)), dma((2, le)), dma((3, le)), dma((3, le)), dma((3, le)), dma((3, le)), dma((2, le)), dma((2, le)), dma, dma,
             ],
             compiler_params=pltpu.CompilerParams(collective_id=0, has_side_effects=True, vmem_limit_bytes=40 * 2**20),
             name="front",
@@ -374,9 +375,9 @@
 
         ends = (sds((n, d_model), BF16), sds((n, d_model), BF16), sds((n_experts, d_model), F32))
         parts = pl.pallas_call(
-            make_back(n_experts, capacity, cap),
+            make_back(cap),
             out_shape=ends,
-            in_specs=[vmem] * 9,
+            in_specs=[vmem] * 11,
             out_specs=(vmem,) * 3,
             scratch_shapes=[
                 pltpu.VMEM((n, half), BF16), pltpu.VMEM((n, half), BF16),
@@ -387,7 +388,7 @@
             ],
             compiler_params=pltpu.CompilerParams(collective_id=1, has_side_effects=True, vmem_limit_bytes=24 * 2**20),
             name="back",
-        )(tokens, grad_out, wgt, idx_row, ynear, yland0, yland1, sown, srecv)
+        )(tokens, grad_out, wgt, picks, prob, chosen, ynear, yland0, yland1, sown, srecv)
         out, dx, dwgt = pl.pallas_call(
             finish, out_shape=ends, in_specs=[vmem] * 3, out_specs=(hbm,) * 3, scratch_shapes=[dma((3,))],
             compiler_params=pltpu.CompilerParams(vmem_limit_bytes=8 * 2**20), name="finish",

time: 60.5 us -> 56.4 us (0.932)
  Pallas kernels: 53.4 us -> 50.5 us
  starting transfers between devices: 3.58 us -> 2.28 us
    pallas_call x1, Pallas kernels: 25.6 us -> 23.1 us  [local_block(): pl.pallas_call(make_front(n_experts, capacity, cap), out_shape=(sds((le,...]
    ppermute x1, starting transfers between devices: 1.54 us -> 0.57 us  [local_block(): srecv = lax.ppermute(speer, 'tp', [(0, 1), (1, 0)])]
  transfers between devices with their start and end apart: 3 -> 3, of which waited for: 1 -> 1; matrix products, arithmetic and copies ran while one was open for 0% -> 0% of each run, Pallas kernels for 19% -> 20%
where the time goes in v4:
time: 56.4 us; the launch traced here: 56.3 us
  Pallas kernels  50.5 us (90%)
  waiting for transfers between devices  2.86 us (5%)
  starting transfers between devices  2.28 us (4%)
  between operations  0.68 us (1%)
    pallas_call x1, Pallas kernels, local_block(): pl.pallas_call(make_front(n_experts, capacity, cap), out_shape=(sds((le,...  23.1 us
    pallas_call x1, Pallas kernels, local_block(): pl.pallas_call(make_back(cap), out_shape=ends, in_specs=[vmem] * 11, out_...  14.9 us
    pallas_call x1, Pallas kernels, local_block(): pl.pallas_call(grads_kernel, grid=(le, steps), out_shape=(sds((le, d_mode...  11.5 us
    ppermute x1, waiting for transfers between devices, local_block(): srecv = lax.ppermute(speer, 'tp', [(0, 1), (1, 0)])  2.86 us
    ppermute x1, starting transfers between devices, local_block(): yland0 = lax.ppermute(yfar0, 'ep', [(0, 2), (2, 0), (1, 3), (3, 1)])  1.49 us
  transfers between devices with their start and end apart: 3, of which 1 were waited for; matrix products, arithmetic and copies ran while one was open for 0% of the time, Pallas kernels for 20%

profile of v4, /device:TPU:0, one launch (start us, length us, event | category | flops | bytes accessed | tf_op | source)
XLA Modules:
  0.0 56.3 jit_solution(3299350629269405368)
XLA Ops:
  0.6 23.1 %front.1 = (bf16[2,160,2048]{2,1,0:T(8,128)(2,1)S(1)}, bf16[2,160,2048]{2,1,0:T(8,128)(2,1)S(1)}, bf16[2,160,1024]{2,1,0:T(8,128)(2,1)S(1)}, bf16[2,160,1024]{2,...) custom-call(bf16[256,1024]{1,0:T(8,128)(2,1)} %x_ref.1, ...), custom_call_target="tpu_custom_call" | custom-call | tf_op jit(solution)/shard_map/front/pallas_call | solution.py:335
  23.8 0.0 copy-start
  23.8 0.0 copy-start.1
  23.8 0.0 copy-start.2
  23.8 0.6 %collective-permute-start.2 = (f32[2,160,512]{2,1,0:T(8,128)S(1)}, f32[2,160,512]{2,1,0:T(8,128)S(1)}, u32[]{:S(2)}, u32[]{:S(2)}) collective-permute-start(f32[2,160,512]{2,1,0:T(8,128)S(1)} %get-tuple-element.32), channel_id=1, source_target_pairs={{0,4},{4,0},{1,5},{5,1},{2,6},{6,2},{3,7},{7,3}} | collective-permute-start | bytes 1966088 | tf_op jit(solution)/shard_map/ppermute | solution.py:357
  24.4 1.5 %collective-permute-start = (bf16[80,512]{1,0:T(8,128)(2,1)S(1)}, bf16[80,512]{1,0:T(8,128)(2,1)S(1)}, u32[]{:S(2)}, u32[]{:S(2)}) collective-permute-start(bf16[80,512]{1,0:T(8,128)(2,1)S(1)} %get-tuple-element.29), channel_id=1, source_target_pairs={{0,2},{2,0},{1,3},{3,1},{4,6},{6,4},{5,7},{7,5}} | collective-permute-start | bytes 245768 | tf_op jit(solution)/shard_map/ppermute | solution.py:358
  25.9 0.2 collective-permute-start.1
  26.1 11.5 %weight_grads.1 = (f32[2,1024,2048]{2,1,0:T(8,128)}, f32[2,2048,1024]{2,1,0:T(8,128)}) custom-call(bf16[2,160,2048]{2,1,0:T(8,128)(2,1)S(1)} %get-tuple-element.38.h_ref, bf16[2,160,1024]{2,1,0:T(8,128)(2,1)S(1)} %get-tuple-element.39.dys_ref, bf16[2,160,1024]{2,1,0:T(8,128)(2,1)S(1)} %get-tuple-element.40.xs_ref, ...), custom_call_target="tpu_custom_call" | custom-call | flops 2684354560 | bytes 33554432 | tf_op jit(solution)/shard_map/weight_grads/pallas_call | solution.py:363
  37.6 0.0 collective-permute-done.yfar0_ref
  37.6 0.0 collective-permute-done.1.yfar1_ref
  37.6 2.9 %collective-permute-done.2.srecv_ref = f32[2,160,512]{2,1,0:T(8,128)S(1)} collective-permute-done((f32[2,160,512]{2,1,0:T(8,128)S(1)}, f32[2,160,512]{2,1,0:T(8,128)S(1)}, u32[]{:S(2)}, u32[]{:S(2)}) %collective-permute-start.2) | collective-permute-done | bytes 655392 | tf_op jit(solution)/shard_map/ppermute | solution.py:357
  40.4 0.0 copy-done
  40.4 0.0 copy-done.1
  40.4 0.0 copy-done.2
  40.4 14.9 %back.1 = (bf16[256,1024]{1,0:T(8,128)(2,1)S(1)}, bf16[256,1024]{1,0:T(8,128)(2,1)S(1)}, f32[8,1024]{1,0:T(8,128)S(1)}) custom-call(bf16[256,1024]{1,0:T(8,128)(2,1)S(1)} %copy-done, bf16[256,1024]{1,0:T(8,128)(2,1)S(1)} %copy-done.1, bf16[8,1024]{1,0:T(8,128)(2,1)S(1)} %bitcast.4, bf16[320,256]{1,0:T(8,128)(2,1)S(1)} %get-tuple-element.25.picks_ref, ...), custom_call_target="tpu_custom_call" | custom-call | tf_op jit(solution)/shard_map/back/pallas_call | solution.py:377
  55.3 1.0 %finish.1 = (bf16[256,1024]{1,0:T(8,128)(2,1)}, bf16[256,1024]{1,0:T(8,128)(2,1)}, f32[8,1024]{1,0:T(8,128)}) custom-call(bf16[256,1024]{1,0:T(8,128)(2,1)S(1)} %get-tuple-element.33.out_ref, bf16[256,1024]{1,0:T(8,128)(2,1)S(1)} %get-tuple-element.34.dx_ref, f32[8,1024]{1,0:T(8,128)S(1)} %get-tuple-element.35.dwgt_ref), custom_call_target="tpu_custom_call" | custom-call | tf_op jit(solution)/shard_map/finish/pallas_call | solution.py:392
Async XLA Ops:
  23.8 16.6 %copy-start = (bf16[256,1024]{1,0:T(8,128)(2,1)S(1)}, bf16[256,1024]{1,0:T(8,128)(2,1)}, u32[]{:S(2)}) copy-start(bf16[256,1024]{1,0:T(8,128)(2,1)} %x_ref.1) | copy-start | bytes 1572868
  23.8 16.6 %copy-start.1 = (bf16[256,1024]{1,0:T(8,128)(2,1)S(1)}, bf16[256,1024]{1,0:T(8,128)(2,1)}, u32[]{:S(2)}) copy-start(bf16[256,1024]{1,0:T(8,128)(2,1)} %gy_ref.1) | copy-start | bytes 1572868
  23.8 16.6 %copy-start.2 = (bf16[1024,8]{0,1:T(8,128)(2,1)S(1)}, bf16[1024,8]{0,1:T(8,128)(2,1)}, u32[]{:S(2)}) copy-start(bf16[1024,8]{0,1:T(8,128)(2,1)} %param.8) | copy-start | bytes 49156
  23.8 16.6 %collective-permute-start.2 = (f32[2,160,512]{2,1,0:T(8,128)S(1)}, f32[2,160,512]{2,1,0:T(8,128)S(1)}, u32[]{:S(2)}, u32[]{:S(2)}) collective-permute-start(f32[2,160,512]{2,1,0:T(8,128)S(1)} %get-tuple-element.32), channel_id=1, source_target_pairs={{0,4},{4,0},{1,5},{5,1},{2,6},{6,2},{3,7},{7,3}} | collective-permute-start | bytes 1966088 | tf_op jit(solution)/shard_map/ppermute | solution.py:357
  24.4 13.2 %collective-permute-start = (bf16[80,512]{1,0:T(8,128)(2,1)S(1)}, bf16[80,512]{1,0:T(8,128)(2,1)S(1)}, u32[]{:S(2)}, u32[]{:S(2)}) collective-permute-start(bf16[80,512]{1,0:T(8,128)(2,1)S(1)} %get-tuple-element.29), channel_id=1, source_target_pairs={{0,2},{2,0},{1,3},{3,1},{4,6},{6,4},{5,7},{7,5}} | collective-permute-start | bytes 245768 | tf_op jit(solution)/shard_map/ppermute | solution.py:358
  25.9 11.7 %collective-permute-start.1 = (bf16[80,512]{1,0:T(8,128)(2,1)S(1)}, bf16[80,512]{1,0:T(8,128)(2,1)S(1)}, u32[]{:S(2)}, u32[]{:S(2)}) collective-permute-start(bf16[80,512]{1,0:T(8,128)(2,1)S(1)} %get-tuple-element.30), channel_id=1, source_target_pairs={{0,3},{3,0},{1,2},{2,1},{4,7},{7,4},{5,6},{6,5}} | collective-permute-start | bytes 245768 | tf_op jit(solution)/shard_map/ppermute | solution.py:359
